TPU v7x, 32 devices: a whole 2x2x4 slice. The times are simulated.
32 devices in a mesh: pp: 4 (over y, x), cp: 8 (over z, core).
Axes of the slice: x: 2, y: 2, z: 4, core: 2. Of those that a mesh axis runs over, the one named last changes fastest.
Arguments:
- x_in: bfloat16 [4, 1024, 2048], P(None, 'cp'), may hold values from -60 to 80
- norm_gain: float32 [4, 2048], P('pp'), may hold values from 0.5 to 1.5
- w_qkv: bfloat16 [4, 2048, 3072], P('pp', 'cp'), may hold values from -0.13258252 to 1.307771
- w_out: bfloat16 [4, 2048, 2048], P('pp', 'cp'), may hold values from -0.125 to 0.125
- cycle_size: int32 [4], replicated, may hold values from 2 to 8, as said below
- token_pos: int32 [4, 1024], replicated, may hold values from 0 to 1023, as said below
- doc_starts: int32 [4, 16], replicated, may hold values from 0 to 1024, as said below
Outputs:
- layer_outputs: bfloat16 [4, 4, 1024, 2048], P('pp', None, 'cp')
Inputs may be any that keep to these rules, and one draw needn't show every extreme that they name: `cycle_size`: powers of two dividing the devices of cp; some micro-batch has 8 and some has 2. `token_pos`: for a micro-batch with group size r, every aligned block of r * 128 slots holds each position of that block once. `doc_starts`: for a micro-batch with group size r and g below 8 / r, entry 2 g is g * r * 128 and entry 2 g + 1 either lies strictly inside that group's positions or is 1024, so each group holds one or two documents; the remaining entries are 1024.
All inputs are finite; a program needn't handle non-finite values.
Results may differ from a plain program's by a relative error of at most 0.0075.
Values may be sent and summed in bfloat16 or wider, within the bound.
No kernel may reach another device: no remote copies, remote signals or barrier semaphores. Data moves between devices by JAX's collectives and lax.ppermute only.
A program may use at most 128 MiB of HBM per device.

v0:
```python
import jax
import jax.numpy as jnp
from jax import lax
from jax.sharding import PartitionSpec as P

HEADS = 16
KV_HEADS = 4
HEAD_DIM = 128
CYCLE_MAX = 8


epsilon = 1e-05
rope_base = 500000.0


def swapped(array, axis, stride):
    return lax.ppermute(array, axis, [(i, i ^ 1 << stride) for i in range(lax.axis_size(axis))])


def from_behind(value, axis, steps):
    count = lax.axis_size(axis)
    leading, last = (max(0, -steps), min(count, count - steps))
    return lax.ppermute(value, axis, [(source, source + steps) for source in range(leading, last)])


def rotate(values, relative):
    half_dim = values.shape[-1] // 2
    frequency_index = jnp.arange(half_dim, dtype=jnp.float32)
    inverse = jnp.power(jnp.float32(rope_base), -2.0 * frequency_index / values.shape[-1])
    angles = relative.astype(jnp.float32)[:, None] * inverse[None, :]
    cosine = jnp.cos(angles)[:, None, :]
    sine_part = jnp.sin(angles)[:, None, :]
    first_half = values[..., :half_dim]
    second_half = values[..., half_dim:]
    return jnp.concatenate(
        [
            first_half * cosine - second_half * sine_part,
            second_half * cosine + first_half * sine_part,
        ],
        axis=-1,
    )


def doc_begin(positions, starts):
    at_or_below = starts[None, :] <= positions[:, None]
    return jnp.max(jnp.where(at_or_below, starts[None, :], 0), axis=1)


def collect_keys(own_piece, device):
    tok_rows, piece_cols = own_piece.shape
    bit_total = CYCLE_MAX.bit_length() - 1
    bit_order = list(reversed(range(bit_total)))
    key_block = own_piece[None]
    for bit_index in bit_order:
        partner = swapped(key_block, "cp", bit_index)
        upper_half = device // (1 << bit_index) % 2 == 1
        key_block = jnp.where(
            upper_half,
            jnp.concatenate([partner, key_block], axis=0),
            jnp.concatenate([key_block, partner], axis=0),
        )
    shaped = key_block.reshape((2,) * bit_total + (tok_rows, piece_cols))
    flipped = tuple(reversed(range(bit_total))) + (bit_total, bit_total + 1)
    key_block = jnp.transpose(shaped, flipped)
    return key_block.reshape(CYCLE_MAX * tok_rows, piece_cols)


def attend_block(queries, key_block, query_pos, key_pos, starts, cycle_devices):
    tok_rows = queries.shape[0]
    key_cols = KV_HEADS * HEAD_DIM
    grouped = queries.reshape(tok_rows, KV_HEADS, HEADS // KV_HEADS, HEAD_DIM)
    key_part = key_block[:, :key_cols].reshape(-1, KV_HEADS, HEAD_DIM)
    value_part = key_block[:, key_cols:].reshape(-1, KV_HEADS, HEAD_DIM)
    scores = jnp.einsum(
        "bkgd,skd->kgbs", grouped, key_part, preferred_element_type=jnp.float32
    ) * HEAD_DIM ** (-0.5)
    span = cycle_devices * tok_rows
    query_begin = doc_begin(query_pos, starts)
    key_begin = doc_begin(key_pos, starts)
    visible = (
        ((query_pos // span)[:, None] == (key_pos // span)[None, :])
        & (query_begin[:, None] == key_begin[None, :])
        & (key_pos[None, :] <= query_pos[:, None])
    )
    scores = jnp.where(visible[None, None], scores, -1e30)
    row_max = jnp.max(scores, axis=-1, keepdims=True)
    weights_exp = jnp.exp(scores - row_max)
    row_sum = jnp.sum(weights_exp, axis=-1, keepdims=True)
    combined = (
        jnp.einsum(
            "kgbs,skd->kgbd",
            weights_exp.astype(jnp.bfloat16),
            value_part,
            preferred_element_type=jnp.float32,
        )
        / row_sum
    )
    return (
        jnp.transpose(combined, (2, 0, 1, 3))
        .reshape(tok_rows, HEADS * HEAD_DIM)
        .astype(jnp.bfloat16)
    )


def body(x_in, norm_gain, w_qkv, w_out, cycle_size, token_pos, doc_starts):
    sections = lax.axis_size("pp")
    section_index = lax.axis_index("pp")
    device = lax.axis_index("cp")
    micro_count, tok_rows, model_width = x_in.shape
    query_cols = HEADS * HEAD_DIM
    key_cols = KV_HEADS * HEAD_DIM
    gain_row = norm_gain[0]
    out_full = None
    qkv_gathered, out_gathered = (
        lax.all_gather(w_qkv, "cp", axis=1, tiled=True),
        lax.all_gather(w_out, "cp", axis=1, tiled=True),
    )
    qkv_full = qkv_gathered[0]
    out_full = out_gathered[0]
    carried = jnp.zeros((tok_rows, model_width), jnp.bfloat16)
    outputs = jnp.zeros((micro_count, tok_rows, model_width), jnp.bfloat16)
    turn_count = micro_count + sections - 1
    for turn_index in range(turn_count):
        offset = turn_index - section_index
        active = (offset >= 0) & (offset < micro_count)
        micro_index = jnp.clip(offset, 0, micro_count - 1)
        fresh_input = lax.dynamic_index_in_dim(x_in, micro_index, 0, keepdims=False)
        hidden = jnp.where(section_index == 0, fresh_input, carried)
        positions = lax.dynamic_index_in_dim(token_pos, micro_index, 0, keepdims=False)
        starts = lax.dynamic_index_in_dim(doc_starts, micro_index, 0, keepdims=False)
        cycle_devices = lax.dynamic_index_in_dim(cycle_size, micro_index, 0, keepdims=False)
        own_pos = lax.dynamic_slice_in_dim(positions, device * tok_rows, tok_rows)

        def front_work(layer_input):
            widened = layer_input.astype(jnp.float32)
            mean_square = jnp.mean(widened * widened, axis=-1, keepdims=True)
            normed = (widened * lax.rsqrt(mean_square + epsilon) * gain_row).astype(jnp.bfloat16)
            projected = jnp.dot(normed, qkv_full, preferred_element_type=jnp.float32)
            relative = own_pos - doc_begin(own_pos, starts)
            queries = rotate(
                projected[:, :query_cols].reshape(tok_rows, HEADS, HEAD_DIM), relative
            ).astype(jnp.bfloat16)
            keys_own = rotate(
                projected[:, query_cols : query_cols + key_cols].reshape(
                    tok_rows, KV_HEADS, HEAD_DIM
                ),
                relative,
            ).astype(jnp.bfloat16)
            values_own = projected[:, query_cols + key_cols :].astype(jnp.bfloat16)
            return (
                queries,
                jnp.concatenate([keys_own.reshape(tok_rows, key_cols), values_own], axis=1),
            )

        def front_empty(layer_input):
            return (
                jnp.zeros((tok_rows, HEADS, HEAD_DIM), jnp.bfloat16),
                jnp.zeros((tok_rows, 2 * key_cols), jnp.bfloat16),
            )

        queries, own_piece = lax.cond(active, front_work, front_empty, hidden)
        key_block = collect_keys(own_piece, device)
        block_start = device // CYCLE_MAX * CYCLE_MAX
        key_pos = lax.dynamic_slice_in_dim(positions, block_start * tok_rows, CYCLE_MAX * tok_rows)
        out_matrix = out_full

        def back_work(layer_input):
            attended = attend_block(queries, key_block, own_pos, key_pos, starts, cycle_devices)
            return (
                layer_input.astype(jnp.float32)
                + jnp.dot(attended, out_matrix, preferred_element_type=jnp.float32)
            ).astype(jnp.bfloat16)

        def back_empty(layer_input):
            return jnp.zeros((tok_rows, model_width), jnp.bfloat16)

        result = lax.cond(active, back_work, back_empty, hidden)
        outputs = jnp.where(
            active, lax.dynamic_update_index_in_dim(outputs, result, micro_index, 0), outputs
        )
        if turn_index + 1 < turn_count:
            carried = from_behind(result, "pp", 1)
    return outputs[None]


def solution(mesh):
    in_specs = (
        P(None, "cp", None),
        P("pp", None),
        P("pp", "cp", None),
        P("pp", "cp", None),
        P(),
        P(),
        P(),
    )
    out_specs = P("pp", None, "cp", None)
    return jax.shard_map(body, mesh=mesh, in_specs=in_specs, out_specs=out_specs, check_vma=False)
```

profile of v0, /device:TPU:7, one launch (start us, length us, event | category | flops | bytes accessed | tf_op | source)
XLA Modules:
  0.0 756.8 jit_solution(12128006746851034836)
XLA Ops:
  12.3 115.0 %all-gather.3.cloned.1.call-done = bf16[1,2048,3072]{2,1,0:T(8,128)(2,1)} async-done(((bf16[1,256,3072]{2,1,0:T(8,128)(2,1)}), bf16[1,2048,3072]{2,1,0:T(8,128)(2,1)}) %all-gather.3.cloned.1.call-update) | async-done | bytes 12582928 | tf_op jit(solution)/shard_map/all_gather | solution.py:115
  127.8 16.6 %collective-permute-done = bf16[1,128,1024]{2,1,0:T(8,128)(2,1)S(1)} collective-permute-done((bf16[1,128,1024]{2,1,0:T(8,128)(2,1)S(1)}, bf16[1,128,1024]{2,1,0:T(8,128)(2,1)S(1)}, u32[]{:S(2)}, u32[]{:S(2)}) %collective-permute-start) | collective-permute-done | bytes 262176 | tf_op jit(solution)/shard_map/ppermute | solution.py:17
  144.6 53.8 %collective-permute-done.1 = bf16[2,128,1024]{2,1,0:T(8,128)(2,1)S(1)} collective-permute-done((bf16[2,128,1024]{2,1,0:T(8,128)(2,1)S(1)}, bf16[2,128,1024]{2,1,0:T(8,128)(2,1)S(1)}, u32[]{:S(2)}, u32[]{:S(2)}) %collective-permute-start.1) | collective-permute-done | bytes 524320 | tf_op jit(solution)/shard_map/ppermute | solution.py:17
  211.8 9.4 %all-gather.5.cloned.1.call-done = bf16[1,2048,2048]{2,1,0:T(8,128)(2,1)} async-done(((bf16[1,256,2048]{2,1,0:T(8,128)(2,1)}), bf16[1,2048,2048]{2,1,0:T(8,128)(2,1)}) %all-gather.5.cloned.1.call-update) | async-done | bytes 8388624 | tf_op jit(solution)/shard_map/all_gather | solution.py:116
  223.5 14.0 %collective-permute-done.3 = bf16[128,2048]{1,0:T(8,128)(2,1)S(1)} collective-permute-done((bf16[128,2048]{1,0:T(8,128)(2,1)}, bf16[128,2048]{1,0:T(8,128)(2,1)S(1)}, u32[]{:S(2)}, u32[]{:S(2)}) %collective-permute-start.3) | collective-permute-done | bytes 524320 | tf_op jit(solution)/shard_map/ppermute | solution.py:23
  241.4 10.9 %collective-permute-done.4 = bf16[1,128,1024]{2,1,0:T(8,128)(2,1)S(1)} collective-permute-done((bf16[1,128,1024]{2,1,0:T(8,128)(2,1)S(1)}, bf16[1,128,1024]{2,1,0:T(8,128)(2,1)S(1)}, u32[]{:S(2)}, u32[]{:S(2)}) %collective-permute-start.4) | collective-permute-done | bytes 262176 | tf_op jit(solution)/shard_map/ppermute | solution.py:17
  253.0 11.0 %collective-permute-done.5 = bf16[2,128,1024]{2,1,0:T(8,128)(2,1)S(1)} collective-permute-done((bf16[2,128,1024]{2,1,0:T(8,128)(2,1)S(1)}, bf16[2,128,1024]{2,1,0:T(8,128)(2,1)S(1)}, u32[]{:S(2)}, u32[]{:S(2)}) %collective-permute-start.5) | collective-permute-done | bytes 524320 | tf_op jit(solution)/shard_map/ppermute | solution.py:17
  279.0 13.9 %collective-permute-done.7 = bf16[128,2048]{1,0:T(8,128)(2,1)S(1)} collective-permute-done((bf16[128,2048]{1,0:T(8,128)(2,1)}, bf16[128,2048]{1,0:T(8,128)(2,1)S(1)}, u32[]{:S(2)}, u32[]{:S(2)}) %collective-permute-start.7) | collective-permute-done | bytes 524320 | tf_op jit(solution)/shard_map/ppermute | solution.py:23
  296.6 11.7 %collective-permute-done.8 = bf16[1,128,1024]{2,1,0:T(8,128)(2,1)S(1)} collective-permute-done((bf16[1,128,1024]{2,1,0:T(8,128)(2,1)S(1)}, bf16[1,128,1024]{2,1,0:T(8,128)(2,1)S(1)}, u32[]{:S(2)}, u32[]{:S(2)}) %collective-permute-start.8) | collective-permute-done | bytes 262176 | tf_op jit(solution)/shard_map/ppermute | solution.py:17
  309.6 10.9 %collective-permute-done.9 = bf16[2,128,1024]{2,1,0:T(8,128)(2,1)S(1)} collective-permute-done((bf16[2,128,1024]{2,1,0:T(8,128)(2,1)S(1)}, bf16[2,128,1024]{2,1,0:T(8,128)(2,1)S(1)}, u32[]{:S(2)}, u32[]{:S(2)}) %collective-permute-start.9) | collective-permute-done | bytes 524320 | tf_op jit(solution)/shard_map/ppermute | solution.py:17
  334.0 11.9 %collective-permute-start.11 = (bf16[128,2048]{1,0:T(8,128)(2,1)}, bf16[128,2048]{1,0:T(8,128)(2,1)S(1)}, u32[]{:S(2)}, u32[]{:S(2)}) collective-permute-start(bf16[128,2048]{1,0:T(8,128)(2,1)} %get-tuple-element.681), channel_id=1, source_target_pairs={{0,8},{8,16},{16,24},{1,9},{9,17},{17,25},{2,10},{10,18},{18,26},{... | collective-permute-start | bytes 1572872 | tf_op jit(solution)/shard_map/ppermute | solution.py:23
  345.8 79.6 %collective-permute-done.11 = bf16[128,2048]{1,0:T(8,128)(2,1)S(1)} collective-permute-done((bf16[128,2048]{1,0:T(8,128)(2,1)}, bf16[128,2048]{1,0:T(8,128)(2,1)S(1)}, u32[]{:S(2)}, u32[]{:S(2)}) %collective-permute-start.11) | collective-permute-done | bytes 524320 | tf_op jit(solution)/shard_map/ppermute | solution.py:23
  426.6 9.0 %conditional.20 = (bf16[128,16,128]{2,1,0:T(8,128)(2,1)S(1)}, bf16[1,128,1024]{2,1,0:T(8,128)(2,1)S(1)}) conditional(s32[]{:T(128)} %convert_element_type.311, () %tuple.184, (bf16[128,2048]{1,0:T(8,128)(2,1)S(1)}, f32[1,2048]{1,0:T(1,128)S(1)}, bf16[2048,3072]{1,0:T(8,128)(2,1)}, s32[16]{0:T(128)S(1)}, s32[128]{0:T(128)S(1)}) %tuple.322), branch_computations={%region_30.31_spmd, %region_31.34_spmd} | conditional | flops 1615608192 | bytes 24983120 | solution.py:161
  436.0 14.0 %collective-permute-done.12 = bf16[1,128,1024]{2,1,0:T(8,128)(2,1)S(1)} collective-permute-done((bf16[1,128,1024]{2,1,0:T(8,128)(2,1)S(1)}, bf16[1,128,1024]{2,1,0:T(8,128)(2,1)S(1)}, u32[]{:S(2)}, u32[]{:S(2)}) %collective-permute-start.12) | collective-permute-done | bytes 262176 | tf_op jit(solution)/shard_map/ppermute | solution.py:17
  450.2 13.0 %collective-permute-done.13 = bf16[2,128,1024]{2,1,0:T(8,128)(2,1)S(1)} collective-permute-done((bf16[2,128,1024]{2,1,0:T(8,128)(2,1)S(1)}, bf16[2,128,1024]{2,1,0:T(8,128)(2,1)S(1)}, u32[]{:S(2)}, u32[]{:S(2)}) %collective-permute-start.13) | collective-permute-done | bytes 524320 | tf_op jit(solution)/shard_map/ppermute | solution.py:17
  473.5 18.7 %conditional.21 = (bf16[128,2048]{1,0:T(8,128)(2,1)}, bf16[1,128,2048]{2,1,0:T(8,128)(2,1)}) conditional(s32[]{:T(128)} %convert_element_type.311, () %tuple.183, (bf16[128,2048]{1,0:T(8,128)(2,1)S(1)}, s32[128]{0:T(128)S(1)}, s32[4]{0:T(128)S(1)}, s32[]{:T(128)}, s32[4,1024]{1,0:T(4,128)S(1)}, /*index=5*/s32[16]{0:T(128)S(1)}, ...), branch_computations={%region_34.35_spmd, %region_35.40_spmd} | conditional | flops 2172577792 | bytes 78724880 | solution.py:177
  493.5 14.8 %collective-permute-done.15 = bf16[128,2048]{1,0:T(8,128)(2,1)S(1)} collective-permute-done((bf16[128,2048]{1,0:T(8,128)(2,1)}, bf16[128,2048]{1,0:T(8,128)(2,1)S(1)}, u32[]{:S(2)}, u32[]{:S(2)}) %collective-permute-start.15) | collective-permute-done | bytes 524320 | tf_op jit(solution)/shard_map/ppermute | solution.py:23
  509.4 9.2 %conditional.22 = (bf16[128,16,128]{2,1,0:T(8,128)(2,1)S(1)}, bf16[1,128,1024]{2,1,0:T(8,128)(2,1)S(1)}) conditional(s32[]{:T(128)} %convert_element_type.312, () %tuple.188, (bf16[128,2048]{1,0:T(8,128)(2,1)S(1)}, f32[1,2048]{1,0:T(1,128)S(1)}, bf16[2048,3072]{1,0:T(8,128)(2,1)}, s32[16]{0:T(128)S(1)}, s32[128]{0:T(128)S(1)}) %tuple.323), branch_computations={%region_40.41_spmd, %region_41.44_spmd} | conditional | flops 1615608192 | bytes 24983120 | solution.py:161
  509.6 6.5 fusion.91
  519.1 14.0 %collective-permute-done.16 = bf16[1,128,1024]{2,1,0:T(8,128)(2,1)S(1)} collective-permute-done((bf16[1,128,1024]{2,1,0:T(8,128)(2,1)S(1)}, bf16[1,128,1024]{2,1,0:T(8,128)(2,1)S(1)}, u32[]{:S(2)}, u32[]{:S(2)}) %collective-permute-start.16) | collective-permute-done | bytes 262176 | tf_op jit(solution)/shard_map/ppermute | solution.py:17
  533.3 13.0 %collective-permute-done.17 = bf16[2,128,1024]{2,1,0:T(8,128)(2,1)S(1)} collective-permute-done((bf16[2,128,1024]{2,1,0:T(8,128)(2,1)S(1)}, bf16[2,128,1024]{2,1,0:T(8,128)(2,1)S(1)}, u32[]{:S(2)}, u32[]{:S(2)}) %collective-permute-start.17) | collective-permute-done | bytes 524320 | tf_op jit(solution)/shard_map/ppermute | solution.py:17
  556.5 18.8 %conditional.23 = (bf16[128,2048]{1,0:T(8,128)(2,1)}, bf16[1,128,2048]{2,1,0:T(8,128)(2,1)}) conditional(s32[]{:T(128)} %convert_element_type.312, () %tuple.187, (bf16[128,2048]{1,0:T(8,128)(2,1)S(1)}, s32[128]{0:T(128)S(1)}, s32[4]{0:T(128)S(1)}, s32[]{:T(128)}, s32[4,1024]{1,0:T(4,128)S(1)}, /*index=5*/s32[16]{0:T(128)S(1)}, ...), branch_computations={%region_44.45_spmd, %region_45.50_spmd} | conditional | flops 2172577792 | bytes 78724880 | solution.py:177
  576.6 14.8 %collective-permute-done.19 = bf16[128,2048]{1,0:T(8,128)(2,1)S(1)} collective-permute-done((bf16[128,2048]{1,0:T(8,128)(2,1)}, bf16[128,2048]{1,0:T(8,128)(2,1)S(1)}, u32[]{:S(2)}, u32[]{:S(2)}) %collective-permute-start.19) | collective-permute-done | bytes 524320 | tf_op jit(solution)/shard_map/ppermute | solution.py:23
  592.5 9.4 %conditional.24 = (bf16[128,16,128]{2,1,0:T(8,128)(2,1)S(1)}, bf16[1,128,1024]{2,1,0:T(8,128)(2,1)S(1)}) conditional(s32[]{:T(128)} %convert_element_type.313, () %tuple.192, (bf16[128,2048]{1,0:T(8,128)(2,1)S(1)}, f32[1,2048]{1,0:T(1,128)S(1)}, bf16[2048,3072]{1,0:T(8,128)(2,1)}, s32[16]{0:T(128)S(1)}, s32[128]{0:T(128)S(1)}) %tuple.342), branch_computations={%region_50.51_spmd, %region_51.54_spmd} | conditional | flops 1615608192 | bytes 24983120 | solution.py:161
  602.4 14.0 %collective-permute-done.20 = bf16[1,128,1024]{2,1,0:T(8,128)(2,1)S(1)} collective-permute-done((bf16[1,128,1024]{2,1,0:T(8,128)(2,1)S(1)}, bf16[1,128,1024]{2,1,0:T(8,128)(2,1)S(1)}, u32[]{:S(2)}, u32[]{:S(2)}) %collective-permute-start.20) | collective-permute-done | bytes 262176 | tf_op jit(solution)/shard_map/ppermute | solution.py:17
  616.6 13.0 %collective-permute-done.21 = bf16[2,128,1024]{2,1,0:T(8,128)(2,1)S(1)} collective-permute-done((bf16[2,128,1024]{2,1,0:T(8,128)(2,1)S(1)}, bf16[2,128,1024]{2,1,0:T(8,128)(2,1)S(1)}, u32[]{:S(2)}, u32[]{:S(2)}) %collective-permute-start.21) | collective-permute-done | bytes 524320 | tf_op jit(solution)/shard_map/ppermute | solution.py:17
  639.8 18.9 %conditional.25 = (bf16[128,2048]{1,0:T(8,128)(2,1)}, bf16[1,128,2048]{2,1,0:T(8,128)(2,1)}) conditional(s32[]{:T(128)} %convert_element_type.313, () %tuple.191, (bf16[128,2048]{1,0:T(8,128)(2,1)S(1)}, s32[128]{0:T(128)S(1)}, s32[4]{0:T(128)S(1)}, s32[]{:T(128)}, s32[4,1024]{1,0:T(4,128)S(1)}, /*index=5*/s32[16]{0:T(128)S(1)}, ...), branch_computations={%region_54.55_spmd, %region_55.60_spmd} | conditional | flops 2172577792 | bytes 78724880 | solution.py:177
  660.0 14.8 %collective-permute-done.23 = bf16[128,2048]{1,0:T(8,128)(2,1)S(1)} collective-permute-done((bf16[128,2048]{1,0:T(8,128)(2,1)}, bf16[128,2048]{1,0:T(8,128)(2,1)S(1)}, u32[]{:S(2)}, u32[]{:S(2)}) %collective-permute-start.23) | collective-permute-done | bytes 524320 | tf_op jit(solution)/shard_map/ppermute | solution.py:23
  676.0 9.2 %conditional.26 = (bf16[128,16,128]{2,1,0:T(8,128)(2,1)S(1)}, bf16[1,128,1024]{2,1,0:T(8,128)(2,1)S(1)}) conditional(s32[]{:T(128)} %convert_element_type.314, () %tuple.196, (bf16[128,2048]{1,0:T(8,128)(2,1)S(1)}, f32[1,2048]{1,0:T(1,128)S(1)}, bf16[2048,3072]{1,0:T(8,128)(2,1)}, s32[16]{0:T(128)S(1)}, s32[128]{0:T(128)S(1)}) %tuple.340), branch_computations={%region_60.61_spmd, %region_61.64_spmd} | conditional | flops 1615608192 | bytes 24983120 | solution.py:161
  686.3 13.4 %collective-permute-done.24 = bf16[1,128,1024]{2,1,0:T(8,128)(2,1)S(1)} collective-permute-done((bf16[1,128,1024]{2,1,0:T(8,128)(2,1)S(1)}, bf16[1,128,1024]{2,1,0:T(8,128)(2,1)S(1)}, u32[]{:S(2)}, u32[]{:S(2)}) %collective-permute-start.24) | collective-permute-done | bytes 262176 | tf_op jit(solution)/shard_map/ppermute | solution.py:17
  700.2 12.6 %collective-permute-done.25 = bf16[2,128,1024]{2,1,0:T(8,128)(2,1)S(1)} collective-permute-done((bf16[2,128,1024]{2,1,0:T(8,128)(2,1)S(1)}, bf16[2,128,1024]{2,1,0:T(8,128)(2,1)S(1)}, u32[]{:S(2)}, u32[]{:S(2)}) %collective-permute-start.25) | collective-permute-done | bytes 524320 | tf_op jit(solution)/shard_map/ppermute | solution.py:17
  721.1 26.7 %conditional.27 = (bf16[1,128,2048]{2,1,0:T(8,128)(2,1)}) conditional(s32[]{:T(128)} %convert_element_type.314, () %tuple.195, (bf16[128,2048]{1,0:T(8,128)(2,1)S(1)}, s32[128]{0:T(128)S(1)}, s32[4]{0:T(128)S(1)}, s32[]{:T(128)}, s32[4,1024]{1,0:T(4,128)S(1)}, /*index=5*/s32[16]{0:T(128)S(1)}, bf16[2,2,2,128,1024]{4,3,0,1,2:T(8,128)(2,1)}, ...), branch_computations={%region_64.65_spmd, %region_65.70_spmd} | conditional | flops 2172577792 | bytes 81870600 | solution.py:177
  (285 shorter events, 225.8 us)
Async XLA Ops:
  6.5 120.8 %all-gather.3.cloned.1.call-start = ((), (), s32[]{:S(2)}) async-start(), calls=%async_computation | async-start | bytes 14155776 | tf_op jit(solution)/shard_map/all_gather | solution.py:115
  7.3 213.9 %all-gather.5.cloned.1.call-start = ((), (), s32[]{:S(2)}) async-start(), calls=%async_computation.1 | async-start | bytes 9437184 | tf_op jit(solution)/shard_map/all_gather | solution.py:116
  127.4 93.7 %copy-start.16 = (s32[4,1024]{1,0:T(4,128)S(1)}, s32[4,1024]{1,0:T(4,128)}, u32[]{:S(2)}) copy-start(s32[4,1024]{1,0:T(4,128)} %param.40) | copy-start | bytes 49156
  127.4 93.7 %copy-start.21 = (s32[4]{0:T(128)S(1)}, s32[4]{0:T(128)}, u32[]{:S(2)}) copy-start(s32[4]{0:T(128)} %param.39) | copy-start | bytes 52
  127.5 16.9 %collective-permute-start = (bf16[1,128,1024]{2,1,0:T(8,128)(2,1)S(1)}, bf16[1,128,1024]{2,1,0:T(8,128)(2,1)S(1)}, u32[]{:S(2)}, u32[]{:S(2)}) collective-permute-start(bf16[1,128,1024]{2,1,0:T(8,128)(2,1)S(1)} %get-tuple-element.670), channel_id=1, source_target_pairs={{0,4},{1,5},{2,6},{3,7},{4,0},{5,1},{6,2},{7,3},{8,12},{9,13},{10,... | collective-permute-start | bytes 786440 | tf_op jit(solution)/shard_map/ppermute | solution.py:17
  144.5 53.9 %collective-permute-start.1 = (bf16[2,128,1024]{2,1,0:T(8,128)(2,1)S(1)}, bf16[2,128,1024]{2,1,0:T(8,128)(2,1)S(1)}, u32[]{:S(2)}, u32[]{:S(2)}) collective-permute-start(bf16[2,128,1024]{2,1,0:T(8,128)(2,1)S(1)} %maximum_select_fusion.14), channel_id=1, source_target_pairs={{0,2},{1,3},{2,0},{3,1},{4,6},{5,7},{6,4},{7,5},{8,10},{9,11},{10,... | collective-permute-start | bytes 1572872 | tf_op jit(solution)/shard_map/ppermute | solution.py:17
  198.5 6.8 collective-permute-start.2
  222.2 15.3 %collective-permute-start.3 = (bf16[128,2048]{1,0:T(8,128)(2,1)}, bf16[128,2048]{1,0:T(8,128)(2,1)S(1)}, u32[]{:S(2)}, u32[]{:S(2)}) collective-permute-start(bf16[128,2048]{1,0:T(8,128)(2,1)} %get-tuple-element.673), channel_id=1, source_target_pairs={{0,8},{8,16},{16,24},{1,9},{9,17},{17,25},{2,10},{10,18},{18,26},{... | collective-permute-start | bytes 1572872 | tf_op jit(solution)/shard_map/ppermute | solution.py:23
  239.0 13.3 %collective-permute-start.4 = (bf16[1,128,1024]{2,1,0:T(8,128)(2,1)S(1)}, bf16[1,128,1024]{2,1,0:T(8,128)(2,1)S(1)}, u32[]{:S(2)}, u32[]{:S(2)}) collective-permute-start(bf16[1,128,1024]{2,1,0:T(8,128)(2,1)S(1)} %get-tuple-element.674), channel_id=1, source_target_pairs={{0,4},{1,5},{2,6},{3,7},{4,0},{5,1},{6,2},{7,3},{8,12},{9,13},{10,... | collective-permute-start | bytes 786440 | tf_op jit(solution)/shard_map/ppermute | solution.py:17
  252.4 11.6 %collective-permute-start.5 = (bf16[2,128,1024]{2,1,0:T(8,128)(2,1)S(1)}, bf16[2,128,1024]{2,1,0:T(8,128)(2,1)S(1)}, u32[]{:S(2)}, u32[]{:S(2)}) collective-permute-start(bf16[2,128,1024]{2,1,0:T(8,128)(2,1)S(1)} %maximum_select_fusion.15), channel_id=1, source_target_pairs={{0,2},{1,3},{2,0},{3,1},{4,6},{5,7},{6,4},{7,5},{8,10},{9,11},{10,... | collective-permute-start | bytes 1572872 | tf_op jit(solution)/shard_map/ppermute | solution.py:17
  264.2 5.2 collective-permute-start.6
  277.7 15.2 %collective-permute-start.7 = (bf16[128,2048]{1,0:T(8,128)(2,1)}, bf16[128,2048]{1,0:T(8,128)(2,1)S(1)}, u32[]{:S(2)}, u32[]{:S(2)}) collective-permute-start(bf16[128,2048]{1,0:T(8,128)(2,1)} %get-tuple-element.677), channel_id=1, source_target_pairs={{0,8},{8,16},{16,24},{1,9},{9,17},{17,25},{2,10},{10,18},{18,26},{... | collective-permute-start | bytes 1572872 | tf_op jit(solution)/shard_map/ppermute | solution.py:23
  294.4 13.9 %collective-permute-start.8 = (bf16[1,128,1024]{2,1,0:T(8,128)(2,1)S(1)}, bf16[1,128,1024]{2,1,0:T(8,128)(2,1)S(1)}, u32[]{:S(2)}, u32[]{:S(2)}) collective-permute-start(bf16[1,128,1024]{2,1,0:T(8,128)(2,1)S(1)} %get-tuple-element.678), channel_id=1, source_target_pairs={{0,4},{1,5},{2,6},{3,7},{4,0},{5,1},{6,2},{7,3},{8,12},{9,13},{10,... | collective-permute-start | bytes 786440 | tf_op jit(solution)/shard_map/ppermute | solution.py:17
  308.4 12.1 %collective-permute-start.9 = (bf16[2,128,1024]{2,1,0:T(8,128)(2,1)S(1)}, bf16[2,128,1024]{2,1,0:T(8,128)(2,1)S(1)}, u32[]{:S(2)}, u32[]{:S(2)}) collective-permute-start(bf16[2,128,1024]{2,1,0:T(8,128)(2,1)S(1)} %maximum_select_fusion.16), channel_id=1, source_target_pairs={{0,2},{1,3},{2,0},{3,1},{4,6},{5,7},{6,4},{7,5},{8,10},{9,11},{10,... | collective-permute-start | bytes 1572872 | tf_op jit(solution)/shard_map/ppermute | solution.py:17
  320.7 4.6 collective-permute-start.10
  334.0 91.5 %collective-permute-start.11 = (bf16[128,2048]{1,0:T(8,128)(2,1)}, bf16[128,2048]{1,0:T(8,128)(2,1)S(1)}, u32[]{:S(2)}, u32[]{:S(2)}) collective-permute-start(bf16[128,2048]{1,0:T(8,128)(2,1)} %get-tuple-element.681), channel_id=1, source_target_pairs={{0,8},{8,16},{16,24},{1,9},{9,17},{17,25},{2,10},{10,18},{18,26},{... | collective-permute-start | bytes 1572872 | tf_op jit(solution)/shard_map/ppermute | solution.py:23
  435.5 14.5 %collective-permute-start.12 = (bf16[1,128,1024]{2,1,0:T(8,128)(2,1)S(1)}, bf16[1,128,1024]{2,1,0:T(8,128)(2,1)S(1)}, u32[]{:S(2)}, u32[]{:S(2)}) collective-permute-start(bf16[1,128,1024]{2,1,0:T(8,128)(2,1)S(1)} %get-tuple-element.682), channel_id=1, source_target_pairs={{0,4},{1,5},{2,6},{3,7},{4,0},{5,1},{6,2},{7,3},{8,12},{9,13},{10,... | collective-permute-start | bytes 786440 | tf_op jit(solution)/shard_map/ppermute | solution.py:17
  450.1 13.1 %collective-permute-start.13 = (bf16[2,128,1024]{2,1,0:T(8,128)(2,1)S(1)}, bf16[2,128,1024]{2,1,0:T(8,128)(2,1)S(1)}, u32[]{:S(2)}, u32[]{:S(2)}) collective-permute-start(bf16[2,128,1024]{2,1,0:T(8,128)(2,1)S(1)} %maximum_select_fusion.17), channel_id=1, source_target_pairs={{0,2},{1,3},{2,0},{3,1},{4,6},{5,7},{6,4},{7,5},{8,10},{9,11},{10,... | collective-permute-start | bytes 1572872 | tf_op jit(solution)/shard_map/ppermute | solution.py:17
  463.4 3.7 collective-permute-start.14
  492.2 16.1 %collective-permute-start.15 = (bf16[128,2048]{1,0:T(8,128)(2,1)}, bf16[128,2048]{1,0:T(8,128)(2,1)S(1)}, u32[]{:S(2)}, u32[]{:S(2)}) collective-permute-start(bf16[128,2048]{1,0:T(8,128)(2,1)} %get-tuple-element.685), channel_id=1, source_target_pairs={{0,8},{8,16},{16,24},{1,9},{9,17},{17,25},{2,10},{10,18},{18,26},{... | collective-permute-start | bytes 1572872 | tf_op jit(solution)/shard_map/ppermute | solution.py:23
  518.6 14.5 %collective-permute-start.16 = (bf16[1,128,1024]{2,1,0:T(8,128)(2,1)S(1)}, bf16[1,128,1024]{2,1,0:T(8,128)(2,1)S(1)}, u32[]{:S(2)}, u32[]{:S(2)}) collective-permute-start(bf16[1,128,1024]{2,1,0:T(8,128)(2,1)S(1)} %get-tuple-element.686), channel_id=1, source_target_pairs={{0,4},{1,5},{2,6},{3,7},{4,0},{5,1},{6,2},{7,3},{8,12},{9,13},{10,... | collective-permute-start | bytes 786440 | tf_op jit(solution)/shard_map/ppermute | solution.py:17
  533.2 13.1 %collective-permute-start.17 = (bf16[2,128,1024]{2,1,0:T(8,128)(2,1)S(1)}, bf16[2,128,1024]{2,1,0:T(8,128)(2,1)S(1)}, u32[]{:S(2)}, u32[]{:S(2)}) collective-permute-start(bf16[2,128,1024]{2,1,0:T(8,128)(2,1)S(1)} %maximum_select_fusion.18), channel_id=1, source_target_pairs={{0,2},{1,3},{2,0},{3,1},{4,6},{5,7},{6,4},{7,5},{8,10},{9,11},{10,... | collective-permute-start | bytes 1572872 | tf_op jit(solution)/shard_map/ppermute | solution.py:17
  546.4 3.7 collective-permute-start.18
  575.3 16.1 %collective-permute-start.19 = (bf16[128,2048]{1,0:T(8,128)(2,1)}, bf16[128,2048]{1,0:T(8,128)(2,1)S(1)}, u32[]{:S(2)}, u32[]{:S(2)}) collective-permute-start(bf16[128,2048]{1,0:T(8,128)(2,1)} %get-tuple-element.689), channel_id=1, source_target_pairs={{0,8},{8,16},{16,24},{1,9},{9,17},{17,25},{2,10},{10,18},{18,26},{... | collective-permute-start | bytes 1572872 | tf_op jit(solution)/shard_map/ppermute | solution.py:23
  601.9 14.5 %collective-permute-start.20 = (bf16[1,128,1024]{2,1,0:T(8,128)(2,1)S(1)}, bf16[1,128,1024]{2,1,0:T(8,128)(2,1)S(1)}, u32[]{:S(2)}, u32[]{:S(2)}) collective-permute-start(bf16[1,128,1024]{2,1,0:T(8,128)(2,1)S(1)} %get-tuple-element.690), channel_id=1, source_target_pairs={{0,4},{1,5},{2,6},{3,7},{4,0},{5,1},{6,2},{7,3},{8,12},{9,13},{10,... | collective-permute-start | bytes 786440 | tf_op jit(solution)/shard_map/ppermute | solution.py:17
  616.5 13.1 %collective-permute-start.21 = (bf16[2,128,1024]{2,1,0:T(8,128)(2,1)S(1)}, bf16[2,128,1024]{2,1,0:T(8,128)(2,1)S(1)}, u32[]{:S(2)}, u32[]{:S(2)}) collective-permute-start(bf16[2,128,1024]{2,1,0:T(8,128)(2,1)S(1)} %maximum_select_fusion.19), channel_id=1, source_target_pairs={{0,2},{1,3},{2,0},{3,1},{4,6},{5,7},{6,4},{7,5},{8,10},{9,11},{10,... | collective-permute-start | bytes 1572872 | tf_op jit(solution)/shard_map/ppermute | solution.py:17
  629.7 3.7 collective-permute-start.22
  639.8 36.2 %copy-start.17 = (s32[128]{0:T(128)S(1)}, s32[128]{0:T(128)}, u32[]{:S(2)}) copy-start(s32[128]{0:T(128)} %get-tuple-element.955) | copy-start | bytes 1540
  658.7 16.1 %collective-permute-start.23 = (bf16[128,2048]{1,0:T(8,128)(2,1)}, bf16[128,2048]{1,0:T(8,128)(2,1)S(1)}, u32[]{:S(2)}, u32[]{:S(2)}) collective-permute-start(bf16[128,2048]{1,0:T(8,128)(2,1)} %get-tuple-element.693), channel_id=1, source_target_pairs={{0,8},{8,16},{16,24},{1,9},{9,17},{17,25},{2,10},{10,18},{18,26},{... | collective-permute-start | bytes 1572872 | tf_op jit(solution)/shard_map/ppermute | solution.py:23
  685.2 14.5 %collective-permute-start.24 = (bf16[1,128,1024]{2,1,0:T(8,128)(2,1)S(1)}, bf16[1,128,1024]{2,1,0:T(8,128)(2,1)S(1)}, u32[]{:S(2)}, u32[]{:S(2)}) collective-permute-start(bf16[1,128,1024]{2,1,0:T(8,128)(2,1)S(1)} %get-tuple-element.694), channel_id=1, source_target_pairs={{0,4},{1,5},{2,6},{3,7},{4,0},{5,1},{6,2},{7,3},{8,12},{9,13},{10,... | collective-permute-start | bytes 786440 | tf_op jit(solution)/shard_map/ppermute | solution.py:17
  699.8 13.1 %collective-permute-start.25 = (bf16[2,128,1024]{2,1,0:T(8,128)(2,1)S(1)}, bf16[2,128,1024]{2,1,0:T(8,128)(2,1)S(1)}, u32[]{:S(2)}, u32[]{:S(2)}) collective-permute-start(bf16[2,128,1024]{2,1,0:T(8,128)(2,1)S(1)} %maximum_select_fusion.20), channel_id=1, source_target_pairs={{0,2},{1,3},{2,0},{3,1},{4,6},{5,7},{6,4},{7,5},{8,10},{9,11},{10,... | collective-permute-start | bytes 1572872 | tf_op jit(solution)/shard_map/ppermute | solution.py:17
  713.0 6.4 collective-permute-start.26
  (22 other events, 260.2 us)
Sparse Core Ops, SparseCore 0:
  9.0 118.2 all-gather.2
  128.9 92.1 all-gather.4
where the time goes:
time: 763 us; the launch traced here: 757 us
  waiting for transfers between devices  514 us (67%)
  local copies, waits for them, and re-layouts  83.7 us (11%)
  matrix products  50 us (7%)
  other arithmetic  46.4 us (6%)
  starting transfers between devices  42.6 us (6%)
  between operations  14.3 us (2%)
    ppermute x21, waiting for transfers between devices, swapped(): lax.ppermute(array, axis, [(i, i ^ 1 << stride) for i in range(lax.axis_s...  236 us
    ppermute x6, waiting for transfers between devices, from_behind(): lax.ppermute(value, axis, [(source, source + steps) for source in range(l...  152 us
    all_gather x1, waiting for transfers between devices, body(): lax.all_gather(w_qkv, 'cp', axis=1, tiled=True)  115 us
    select_n x6, local copies, waits for them, and re-layouts, collect_keys(): jnp.where(upper_half, jnp.concatenate([partner, key_block], axis=0), jnp....  28.5 us
    dot_general x4, matrix products, front_work(): projected = jnp.dot(normed, qkv_full, preferred_element_type=jnp.float32)  26 us
    ppermute x21, starting transfers between devices, swapped(): lax.ppermute(array, axis, [(i, i ^ 1 << stride) for i in range(lax.axis_s...  24.2 us
    ppermute x6, starting transfers between devices, from_behind(): lax.ppermute(value, axis, [(source, source + steps) for source in range(l...  18.3 us
  transfers between devices with their start and end apart: 29, of which 28 were waited for; matrix products, arithmetic and copies ran while one was open for 2% of the time, Pallas kernels for 0%

commit v1 on v0

v1 whole, which is shorter than its diff:
```python
import functools
import math

import jax
import jax.numpy as jnp
from jax import lax
from jax.experimental import pallas as pl
from jax.experimental.pallas import tpu as pltpu
from jax.sharding import PartitionSpec as P

HEADS = 16
KV_HEADS = 4
HEAD_DIM = 128
CYCLE_MAX = 8
GROUP = HEADS // KV_HEADS
QUERY_COLS = HEADS * HEAD_DIM
KEY_COLS = KV_HEADS * HEAD_DIM

epsilon = 1e-05
rope_base = 500000.0


def swapped(array, bit):
    return lax.ppermute(array, "cp", [(i, i ^ 1 << bit) for i in range(lax.axis_size("cp"))])


def rotate_heads(values, cosine, sine):
    heads = []
    for h in range(values.shape[-1] // HEAD_DIM):
        head = values[:, h * HEAD_DIM : (h + 1) * HEAD_DIM]
        heads.append(head * cosine + pltpu.roll(head, HEAD_DIM // 2, 1) * sine)
    return jnp.concatenate(heads, axis=1)


def kv_kernel(mi_ref, hidden_ref, gain_ref, w_ref, cos_ref, sin_ref, key_ref, value_ref, normed_ref):
    step = pl.program_id(0)

    @pl.when(step == 0)
    def _():
        widened = hidden_ref[...].astype(jnp.float32)
        mean_square = jnp.mean(widened * widened, axis=-1, keepdims=True)
        normed_ref[...] = (widened * lax.rsqrt(mean_square + epsilon) * gain_ref[...]).astype(jnp.bfloat16)

    projected = jnp.dot(normed_ref[...], w_ref[...], preferred_element_type=jnp.float32)

    @pl.when(step == 0)
    def _():
        key_ref[...] = rotate_heads(projected, cos_ref[0], sin_ref[0]).astype(jnp.bfloat16)

    @pl.when(step == 1)
    def _():
        value_ref[...] = projected.astype(jnp.bfloat16)


def query_kernel(mi_ref, normed_ref, w_ref, cos_ref, sin_ref, query_ref):
    projected = jnp.dot(normed_ref[...], w_ref[...], preferred_element_type=jnp.float32)
    query_ref[...] = rotate_heads(projected, cos_ref[0], sin_ref[0]).astype(jnp.bfloat16)


def back_kernel(
    mi_ref, query_ref, *refs
):
    count = (len(refs) - 9) // 2
    key_refs, value_refs = refs[:count], refs[count : 2 * count]
    qcode_ref, qpos_ref, kcode_ref, kpos_ref, hidden_ref, w_ref, out_ref, acc_ref, bias_ref = refs[2 * count :]
    step = pl.program_id(0)

    @pl.when(step == 0)
    def _():
        visible = (qcode_ref[0] == kcode_ref[0]) & (kpos_ref[0] <= qpos_ref[0])
        bias_ref[...] = jnp.where(visible, 0.0, -1e30).astype(jnp.float32)
        acc_ref[...] = hidden_ref[...].astype(jnp.float32)

    part = key_refs[0].shape[0]
    factor = HEAD_DIM ** (-0.5) * math.log2(math.e)
    heads = []
    for g in range(GROUP):
        query = query_ref[:, g * HEAD_DIM : (g + 1) * HEAD_DIM]
        scores = [
            lax.dot_general(query, ref[...], (((1,), (1,)), ((), ())), preferred_element_type=jnp.float32)
            + bias_ref[:, i * part : (i + 1) * part]
            for i, ref in enumerate(key_refs)
        ]
        row_max = functools.reduce(jnp.maximum, [jnp.max(s, axis=-1, keepdims=True) for s in scores])
        exps = [jnp.exp2((s - row_max) * factor) for s in scores]
        row_sum = sum(jnp.sum(e, axis=-1, keepdims=True) for e in exps)
        combined = sum(
            jnp.dot(e.astype(jnp.bfloat16), ref[...], preferred_element_type=jnp.float32)
            for e, ref in zip(exps, value_refs)
        )
        heads.append((combined / row_sum).astype(jnp.bfloat16))
    attended = jnp.concatenate(heads, axis=1)
    acc_ref[...] += jnp.dot(attended, w_ref[...], preferred_element_type=jnp.float32)

    @pl.when(step == KV_HEADS - 1)
    def _():
        out_ref[...] = acc_ref[...].astype(jnp.bfloat16)


def call(kernel, grid, in_specs, out_specs, out_shape, scratch=(), name=None):
    return pl.pallas_call(
        kernel,
        grid_spec=pltpu.PrefetchScalarGridSpec(
            num_scalar_prefetch=1,
            grid=(grid,),
            in_specs=in_specs,
            out_specs=out_specs,
            scratch_shapes=scratch,
        ),
        out_shape=out_shape,
        name=name,
    )


def whole_spec(shape):
    return pl.BlockSpec(shape, lambda j, mi: (0,) * len(shape))


def micro_spec(shape):
    return pl.BlockSpec((1,) + shape, lambda j, mi: (mi[0],) + (0,) * len(shape))


def project_kv(mi, hidden, gain, weight, cosine, sine):
    rows, width = hidden.shape
    first = QUERY_COLS // KEY_COLS
    return call(
        kv_kernel,
        2,
        [
            whole_spec((rows, width)),
            whole_spec((1, width)),
            pl.BlockSpec((width, KEY_COLS), lambda j, mi: (0, first + j)),
            micro_spec((rows, HEAD_DIM)),
            micro_spec((rows, HEAD_DIM)),
        ],
        [whole_spec((rows, KEY_COLS)), whole_spec((rows, KEY_COLS)), whole_spec((rows, width))],
        [
            jax.ShapeDtypeStruct((rows, KEY_COLS), jnp.bfloat16),
            jax.ShapeDtypeStruct((rows, KEY_COLS), jnp.bfloat16),
            jax.ShapeDtypeStruct((rows, width), jnp.bfloat16),
        ],
        name="project_kv",
    )(mi, hidden, gain, weight, cosine, sine)


def project_query(mi, normed, weight, cosine, sine):
    rows, width = normed.shape
    cols = QUERY_COLS // 4
    return call(
        query_kernel,
        4,
        [
            whole_spec((rows, width)),
            pl.BlockSpec((width, cols), lambda j, mi: (0, j)),
            micro_spec((rows, HEAD_DIM)),
            micro_spec((rows, HEAD_DIM)),
        ],
        pl.BlockSpec((rows, cols), lambda j, mi: (0, j)),
        jax.ShapeDtypeStruct((rows, QUERY_COLS), jnp.bfloat16),
        name="project_query",
    )(mi, normed, weight, cosine, sine)


def attend_out(mi, query, keys, values, tables, hidden, weight):
    rows, width = hidden.shape
    cols = GROUP * HEAD_DIM
    key_rows = sum(k.shape[0] for k in keys)
    kv_specs = [pl.BlockSpec((k.shape[0], HEAD_DIM), lambda j, mi: (0, j)) for k in keys]
    return call(
        back_kernel,
        KV_HEADS,
        [pl.BlockSpec((rows, cols), lambda j, mi: (0, j))]
        + kv_specs
        + kv_specs
        + [
            micro_spec((rows, 1)),
            micro_spec((rows, 1)),
            micro_spec((1, key_rows)),
            micro_spec((1, key_rows)),
            whole_spec((rows, width)),
            pl.BlockSpec((cols, width), lambda j, mi: (j, 0)),
        ],
        whole_spec((rows, width)),
        jax.ShapeDtypeStruct((rows, width), jnp.bfloat16),
        scratch=[pltpu.VMEM((rows, width), jnp.float32), pltpu.VMEM((rows, key_rows), jnp.float32)],
        name="attend_out",
    )(mi, query, *keys, *values, *tables, hidden, weight)


def collect(own):
    block = own
    for bit in reversed(range(1, CYCLE_MAX.bit_length() - 1)):
        block = jnp.concatenate([block, swapped(block, bit)], axis=0)
    return [block, swapped(block, 0)]


def key_order():
    order = [0]
    for bit in reversed(range(CYCLE_MAX.bit_length() - 1)):
        order = order + [b ^ 1 << bit for b in order]
    return order


def body(x_in, norm_gain, w_qkv, w_out, cycle_size, token_pos, doc_starts):
    sections = lax.axis_size("pp")
    section_index = lax.axis_index("pp")
    device = lax.axis_index("cp")
    micro_count, tok_rows, model_width = x_in.shape
    tokens = token_pos.shape[1]

    begins = jnp.max(
        jnp.where(doc_starts[:, None, :] <= token_pos[:, :, None], doc_starts[:, None, :], 0), axis=2
    )
    codes = token_pos // (cycle_size * tok_rows)[:, None] * tokens + begins
    by_device = lambda a: a.reshape(micro_count, tokens // tok_rows, tok_rows)
    pos_blocks, begin_blocks, code_blocks = by_device(token_pos), by_device(begins), by_device(codes)
    take = lambda a, b: lax.dynamic_index_in_dim(a, device ^ b, 1, keepdims=False)
    own_pos, own_begin, own_code = take(pos_blocks, 0), take(begin_blocks, 0), take(code_blocks, 0)
    order = key_order()
    key_pos = jnp.concatenate([take(pos_blocks, b) for b in order], axis=1)[:, None, :]
    key_code = jnp.concatenate([take(code_blocks, b) for b in order], axis=1)[:, None, :]
    tables = (own_code[:, :, None], own_pos[:, :, None], key_code, key_pos)
    half_dim = HEAD_DIM // 2
    inverse = jnp.power(
        jnp.float32(rope_base), -2.0 * jnp.arange(half_dim, dtype=jnp.float32) / HEAD_DIM
    )
    angles = (own_pos - own_begin).astype(jnp.float32)[:, :, None] * inverse
    cos_half, sin_half = jnp.cos(angles), jnp.sin(angles)
    cosine = jnp.concatenate([cos_half, cos_half], axis=-1)
    sine = jnp.concatenate([-sin_half, sin_half], axis=-1)

    qkv_full = lax.all_gather(w_qkv, "cp", axis=1, tiled=True)[0]
    out_full = lax.all_gather(w_out, "cp", axis=1, tiled=True)[0]

    outputs = jnp.zeros((micro_count, tok_rows, model_width), jnp.bfloat16)
    carried = None
    turn_count = micro_count + sections - 1
    for turn in range(turn_count):
        offset = turn - section_index
        micro_index = jnp.clip(offset, 0, micro_count - 1)
        mi = micro_index.astype(jnp.int32).reshape(1)
        if turn == 0:
            hidden = x_in[0]
        elif turn < micro_count:
            hidden = jnp.where(section_index == 0, x_in[turn], carried)
        else:
            hidden = carried
        key_own, value_own, normed = project_kv(mi, hidden, norm_gain, qkv_full, cosine, sine)
        keys, values = collect(key_own), collect(value_own)
        query = project_query(mi, normed, qkv_full, cosine, sine)
        result = attend_out(mi, query, keys, values, tables, hidden, out_full)
        if turn + 1 < turn_count:
            carried = lax.ppermute(result, "pp", [(i, i + 1) for i in range(sections - 1)])
        kept = result
        if turn >= micro_count:
            kept = jnp.where(offset < micro_count, result, outputs[micro_count - 1])
        outputs = lax.dynamic_update_index_in_dim(outputs, kept, micro_index, 0)
    return outputs[None]


def solution(mesh):
    in_specs = (
        P(None, "cp", None),
        P("pp", None),
        P("pp", "cp", None),
        P("pp", "cp", None),
        P(),
        P(),
        P(),
    )
    out_specs = P("pp", None, "cp", None)
    return jax.shard_map(body, mesh=mesh, in_specs=in_specs, out_specs=out_specs, check_vma=False)
```

time: 763 us -> 641 us (0.84)
  Pallas kernels: 0 us -> 147 us
  waiting for transfers between devices: 514 us -> 377 us
  local copies, waits for them, and re-layouts: 83.7 us -> 27.2 us
  matrix products: 50 us -> 0 us
  other arithmetic: 46.4 us -> 20.8 us
  starting transfers between devices: 42.6 us -> 53.3 us
    pallas_call x0 -> x21, Pallas kernels: none -> 147 us  [the longest x7 76.5 us: attend_out(): call(back_kernel, KV_HEADS, [pl.BlockSpec((rows, cols), lambda j, mi: (0,...]
    ppermute x27 -> x48, waiting for transfers between devices: 388 us -> 255 us  [the longest x42 167 us: swapped(): lax.ppermute(array, 'cp', [(i, i ^ 1 << bit) for i in range(lax.axis_size...]
    dot_general x16 -> x0, matrix products: 50 us -> none  [the longest x4 26 us: front_work(): projected = jnp.dot(normed, qkv_full, preferred_element_type=jnp.float32)]
    select_n x6 -> x0, local copies, waits for them, and re-layouts: 28.5 us -> none  [collect_keys(): jnp.where(upper_half, jnp.concatenate([partner, key_block], axis=0), jnp....]
    select_n x43 -> x3, other arithmetic: 27.9 us -> 2.55 us  [body(): hidden = jnp.where(section_index == 0, x_in[turn], carried)]
    unnamed x27 -> x102, local copies, waits for them, and re-layouts: 1.64 us -> 21.9 us
    reshape x8 -> x0, local copies, waits for them, and re-layouts: 12.9 us -> none  [the longest x4 12.5 us: collect_keys(): return key_block.reshape(CYCLE_MAX * tok_rows, piece_cols)]
    concatenate x8 -> x17, other arithmetic: 1.9 us -> 14.6 us  [the longest x14 12.9 us: collect(): block = jnp.concatenate([block, swapped(block, bit)], axis=0)]
  transfers between devices with their start and end apart: 29 -> 50, of which waited for: 28 -> 36; matrix products, arithmetic and copies ran while one was open for 2% -> 6% of each run, Pallas kernels for 0% -> 7%
where the time goes in v1:
time: 641 us; the launch traced here: 639 us
  waiting for transfers between devices  377 us (59%)
  Pallas kernels  147 us (23%)
  starting transfers between devices  53.3 us (8%)
  local copies, waits for them, and re-layouts  27.2 us (4%)
  other arithmetic  20.8 us (3%)
  between operations  14.3 us (2%)
    ppermute x42, waiting for transfers between devices, swapped(): lax.ppermute(array, 'cp', [(i, i ^ 1 << bit) for i in range(lax.axis_size...  167 us
    all_gather x1, waiting for transfers between devices, body(): qkv_full = lax.all_gather(w_qkv, 'cp', axis=1, tiled=True)[0]  113 us
    ppermute x6, waiting for transfers between devices, body(): lax.ppermute(result, 'pp', [(i, i + 1) for i in range(sections - 1)])  87.7 us
    pallas_call x7, Pallas kernels, attend_out(): call(back_kernel, KV_HEADS, [pl.BlockSpec((rows, cols), lambda j, mi: (0,...  76.5 us
    ppermute x42, starting transfers between devices, swapped(): lax.ppermute(array, 'cp', [(i, i ^ 1 << bit) for i in range(lax.axis_size...  45 us
    pallas_call x7, Pallas kernels, project_query(): call(query_kernel, 4, [whole_spec((rows, width)), pl.BlockSpec((width, co...  42.5 us
    pallas_call x7, Pallas kernels, project_kv(): call(kv_kernel, 2, [whole_spec((rows, width)), whole_spec((1, width)), pl...  27.6 us
    unnamed x102, local copies, waits for them, and re-layouts  21.9 us
  transfers between devices with their start and end apart: 50, of which 36 were waited for; matrix products, arithmetic and copies ran while one was open for 6% of the time, Pallas kernels for 7%

profile of v1, /device:TPU:7, one launch (start us, length us, event | category | flops | bytes accessed | tf_op | source)
XLA Modules:
  0.0 639.2 jit_solution(2139831643233858137)
XLA Ops:
  14.1 113.2 %all-gather.3.cloned.1.call-done = bf16[1,2048,3072]{2,1,0:T(8,128)(2,1)} async-done(((bf16[1,256,3072]{2,1,0:T(8,128)(2,1)}), bf16[1,2048,3072]{2,1,0:T(8,128)(2,1)}) %all-gather.3.cloned.1.call-update) | async-done | bytes 12582928 | tf_op jit(solution)/shard_map/all_gather | solution.py:232
  135.6 13.8 %collective-permute-done = bf16[128,512]{1,0:T(8,128)(2,1)S(1)} collective-permute-done((bf16[128,512]{1,0:T(8,128)(2,1)}, bf16[128,512]{1,0:T(8,128)(2,1)S(1)}, u32[]{:S(2)}, u32[]{:S(2)}) %collective-permute-start) | collective-permute-done | bytes 131104 | tf_op jit(solution)/shard_map/ppermute | solution.py:24
  150.4 7.5 %collective-permute-done.3 = bf16[128,512]{1,0:T(8,128)(2,1)S(1)} collective-permute-done((bf16[128,512]{1,0:T(8,128)(2,1)}, bf16[128,512]{1,0:T(8,128)(2,1)S(1)}, u32[]{:S(2)}, u32[]{:S(2)}) %collective-permute-start.3) | collective-permute-done | bytes 131104 | tf_op jit(solution)/shard_map/ppermute | solution.py:24
  158.9 27.5 %collective-permute-done.1 = bf16[256,512]{1,0:T(8,128)(2,1)S(1)} collective-permute-done((bf16[256,512]{1,0:T(8,128)(2,1)S(1)}, bf16[256,512]{1,0:T(8,128)(2,1)S(1)}, u32[]{:S(2)}, u32[]{:S(2)}) %collective-permute-start.1) | collective-permute-done | bytes 262176 | tf_op jit(solution)/shard_map/ppermute | solution.py:24
  187.6 20.2 %collective-permute-done.4 = bf16[256,512]{1,0:T(8,128)(2,1)S(1)} collective-permute-done((bf16[256,512]{1,0:T(8,128)(2,1)S(1)}, bf16[256,512]{1,0:T(8,128)(2,1)S(1)}, u32[]{:S(2)}, u32[]{:S(2)}) %collective-permute-start.4) | collective-permute-done | bytes 262176 | tf_op jit(solution)/shard_map/ppermute | solution.py:24
  210.0 6.3 project_query.7.query_ref
  216.3 7.7 %all-gather.5.cloned.1.call-done = bf16[1,2048,2048]{2,1,0:T(8,128)(2,1)} async-done(((bf16[1,256,2048]{2,1,0:T(8,128)(2,1)}), bf16[1,2048,2048]{2,1,0:T(8,128)(2,1)}) %all-gather.5.cloned.1.call-update) | async-done | bytes 8388624 | tf_op jit(solution)/shard_map/all_gather | solution.py:233
  224.0 10.9 %attend_out.7 = bf16[128,2048]{1,0:T(8,128)(2,1)} custom-call(s32[1]{0:T(128)} %bitcast.mi_ref, bf16[128,2048]{1,0:T(8,128)(2,1)} %project_query.7.query_ref, bf16[512,512]{1,0:T(8,128)(2,1)} %copy-done.10, bf16[512,512]{1,0:T(8,128)(2,1)} %collective-permute-done.2.refs_1_, bf16[512,512]{1,0:T(8,128)(2,1)} %copy-done.17, ...), custom_call_target="tpu_custom_call" | custom-call | tf_op jit(solution)/shard_map/attend_out/pallas_call | solution.py:169
  236.2 14.0 %collective-permute-done.6 = bf16[128,2048]{1,0:T(8,128)(2,1)S(1)} collective-permute-done((bf16[128,2048]{1,0:T(8,128)(2,1)}, bf16[128,2048]{1,0:T(8,128)(2,1)S(1)}, u32[]{:S(2)}, u32[]{:S(2)}) %collective-permute-start.6) | collective-permute-done | bytes 524320 | tf_op jit(solution)/shard_map/ppermute | solution.py:253
  259.4 6.7 %collective-permute-done.7 = bf16[128,512]{1,0:T(8,128)(2,1)S(1)} collective-permute-done((bf16[128,512]{1,0:T(8,128)(2,1)}, bf16[128,512]{1,0:T(8,128)(2,1)S(1)}, u32[]{:S(2)}, u32[]{:S(2)}) %collective-permute-start.7) | collective-permute-done | bytes 131104 | tf_op jit(solution)/shard_map/ppermute | solution.py:24
  281.5 6.0 project_query.8.query_ref
  287.5 11.0 %attend_out.8 = bf16[128,2048]{1,0:T(8,128)(2,1)} custom-call(s32[1]{0:T(128)} %bitcast.27.mi_ref, bf16[128,2048]{1,0:T(8,128)(2,1)} %project_query.8.query_ref, bf16[512,512]{1,0:T(8,128)(2,1)} %copy-done.11, bf16[512,512]{1,0:T(8,128)(2,1)} %collective-permute-done.9.refs_1_, bf16[512,512]{1,0:T(8,128)(2,1)} %copy-done.18, ...), custom_call_target="tpu_custom_call" | custom-call | tf_op jit(solution)/shard_map/attend_out/pallas_call | solution.py:169
  299.9 14.0 %collective-permute-done.13 = bf16[128,2048]{1,0:T(8,128)(2,1)S(1)} collective-permute-done((bf16[128,2048]{1,0:T(8,128)(2,1)}, bf16[128,2048]{1,0:T(8,128)(2,1)S(1)}, u32[]{:S(2)}, u32[]{:S(2)}) %collective-permute-start.13) | collective-permute-done | bytes 524320 | tf_op jit(solution)/shard_map/ppermute | solution.py:253
  323.0 7.5 %collective-permute-done.14 = bf16[128,512]{1,0:T(8,128)(2,1)S(1)} collective-permute-done((bf16[128,512]{1,0:T(8,128)(2,1)}, bf16[128,512]{1,0:T(8,128)(2,1)S(1)}, u32[]{:S(2)}, u32[]{:S(2)}) %collective-permute-start.14) | collective-permute-done | bytes 131104 | tf_op jit(solution)/shard_map/ppermute | solution.py:24
  346.0 6.0 project_query.9.query_ref
  352.1 10.9 %attend_out.9 = bf16[128,2048]{1,0:T(8,128)(2,1)} custom-call(s32[1]{0:T(128)} %bitcast.30.mi_ref, bf16[128,2048]{1,0:T(8,128)(2,1)} %project_query.9.query_ref, bf16[512,512]{1,0:T(8,128)(2,1)} %copy-done.12, bf16[512,512]{1,0:T(8,128)(2,1)} %collective-permute-done.16.refs_1_, bf16[512,512]{1,0:T(8,128)(2,1)} %copy-done.19, ...), custom_call_target="tpu_custom_call" | custom-call | tf_op jit(solution)/shard_map/attend_out/pallas_call | solution.py:169
  364.3 15.1 %collective-permute-done.20 = bf16[128,2048]{1,0:T(8,128)(2,1)S(1)} collective-permute-done((bf16[128,2048]{1,0:T(8,128)(2,1)}, bf16[128,2048]{1,0:T(8,128)(2,1)S(1)}, u32[]{:S(2)}, u32[]{:S(2)}) %collective-permute-start.20) | collective-permute-done | bytes 524320 | tf_op jit(solution)/shard_map/ppermute | solution.py:253
  388.5 7.5 %collective-permute-done.21 = bf16[128,512]{1,0:T(8,128)(2,1)S(1)} collective-permute-done((bf16[128,512]{1,0:T(8,128)(2,1)}, bf16[128,512]{1,0:T(8,128)(2,1)S(1)}, u32[]{:S(2)}, u32[]{:S(2)}) %collective-permute-start.21) | collective-permute-done | bytes 131104 | tf_op jit(solution)/shard_map/ppermute | solution.py:24
  411.5 6.1 project_query.10.query_ref
  419.1 10.9 %attend_out.10 = bf16[128,2048]{1,0:T(8,128)(2,1)} custom-call(s32[1]{0:T(128)} %bitcast.33.mi_ref, bf16[128,2048]{1,0:T(8,128)(2,1)} %project_query.10.query_ref, bf16[512,512]{1,0:T(8,128)(2,1)} %copy-done.13, bf16[512,512]{1,0:T(8,128)(2,1)} %copy-done.25, bf16[512,512]{1,0:T(8,128)(2,1)} %copy-done.20, bf16[512,512]{1,0:T(8,128)(2,1)} %copy-done.26, ...), custom_call_target="tpu_custom_call" | custom-call | tf_op jit(solution)/shard_map/attend_out/pallas_call | solution.py:169
  431.3 15.1 %collective-permute-done.27.hidden_ref.refs_8_ = bf16[128,2048]{1,0:T(8,128)(2,1)S(1)} collective-permute-done((bf16[128,2048]{1,0:T(8,128)(2,1)}, bf16[128,2048]{1,0:T(8,128)(2,1)S(1)}, u32[]{:S(2)}, u32[]{:S(2)}) %collective-permute-start.27) | collective-permute-done | bytes 524320 | tf_op jit(solution)/shard_map/ppermute | solution.py:253
  455.5 7.5 %collective-permute-done.28 = bf16[128,512]{1,0:T(8,128)(2,1)S(1)} collective-permute-done((bf16[128,512]{1,0:T(8,128)(2,1)}, bf16[128,512]{1,0:T(8,128)(2,1)S(1)}, u32[]{:S(2)}, u32[]{:S(2)}) %collective-permute-start.28) | collective-permute-done | bytes 131104 | tf_op jit(solution)/shard_map/ppermute | solution.py:24
  478.4 6.0 project_query.11.query_ref
  486.1 10.9 %attend_out.11 = bf16[128,2048]{1,0:T(8,128)(2,1)} custom-call(s32[1]{0:T(128)} %bitcast.36.mi_ref, bf16[128,2048]{1,0:T(8,128)(2,1)} %project_query.11.query_ref, bf16[512,512]{1,0:T(8,128)(2,1)} %copy-done.14, bf16[512,512]{1,0:T(8,128)(2,1)} %copy-done.23, bf16[512,512]{1,0:T(8,128)(2,1)} %copy-done.21, bf16[512,512]{1,0:T(8,128)(2,1)} %copy-done.24, ...), custom_call_target="tpu_custom_call" | custom-call | tf_op jit(solution)/shard_map/attend_out/pallas_call | solution.py:169
  499.1 14.5 %collective-permute-done.34.hidden_ref.refs_8_ = bf16[128,2048]{1,0:T(8,128)(2,1)S(1)} collective-permute-done((bf16[128,2048]{1,0:T(8,128)(2,1)}, bf16[128,2048]{1,0:T(8,128)(2,1)S(1)}, u32[]{:S(2)}, u32[]{:S(2)}) %collective-permute-start.34) | collective-permute-done | bytes 524320 | tf_op jit(solution)/shard_map/ppermute | solution.py:253
  523.3 6.9 %collective-permute-done.35 = bf16[128,512]{1,0:T(8,128)(2,1)S(1)} collective-permute-done((bf16[128,512]{1,0:T(8,128)(2,1)}, bf16[128,512]{1,0:T(8,128)(2,1)S(1)}, u32[]{:S(2)}, u32[]{:S(2)}) %collective-permute-start.35) | collective-permute-done | bytes 131104 | tf_op jit(solution)/shard_map/ppermute | solution.py:24
  546.3 6.1 project_query.12.query_ref
  552.4 11.0 %attend_out.12 = bf16[128,2048]{1,0:T(8,128)(2,1)} custom-call(s32[1]{0:T(128)} %bitcast.39.mi_ref, bf16[128,2048]{1,0:T(8,128)(2,1)} %project_query.12.query_ref, bf16[512,512]{1,0:T(8,128)(2,1)} %copy-done.15, bf16[512,512]{1,0:T(8,128)(2,1)} %collective-permute-done.37.refs_1_, bf16[512,512]{1,0:T(8,128)(2,1)} %constant_dynamic-update-slice_fusion.49.refs_2_, ...), custom_call_target="tpu_custom_call" | custom-call | tf_op jit(solution)/shard_map/attend_out/pallas_call | solution.py:169
  564.8 15.1 %collective-permute-done.41.hidden_ref.refs_8_ = bf16[128,2048]{1,0:T(8,128)(2,1)S(1)} collective-permute-done((bf16[128,2048]{1,0:T(8,128)(2,1)}, bf16[128,2048]{1,0:T(8,128)(2,1)S(1)}, u32[]{:S(2)}, u32[]{:S(2)}) %collective-permute-start.41) | collective-permute-done | bytes 524320 | tf_op jit(solution)/shard_map/ppermute | solution.py:253
  589.0 7.6 %collective-permute-done.42 = bf16[128,512]{1,0:T(8,128)(2,1)S(1)} collective-permute-done((bf16[128,512]{1,0:T(8,128)(2,1)}, bf16[128,512]{1,0:T(8,128)(2,1)S(1)}, u32[]{:S(2)}, u32[]{:S(2)}) %collective-permute-start.42) | collective-permute-done | bytes 131104 | tf_op jit(solution)/shard_map/ppermute | solution.py:24
  613.5 6.0 project_query.13.query_ref
  619.5 10.9 %attend_out.13 = bf16[128,2048]{1,0:T(8,128)(2,1)} custom-call(s32[1]{0:T(128)} %bitcast.43.mi_ref, bf16[128,2048]{1,0:T(8,128)(2,1)} %project_query.13.query_ref, bf16[512,512]{1,0:T(8,128)(2,1)} %copy-done.16, bf16[512,512]{1,0:T(8,128)(2,1)} %collective-permute-done.44.refs_1_, bf16[512,512]{1,0:T(8,128)(2,1)} %copy-done.22, ...), custom_call_target="tpu_custom_call" | custom-call | tf_op jit(solution)/shard_map/attend_out/pallas_call | solution.py:169
  (249 shorter events, 184.7 us)
Async XLA Ops:
  6.5 120.8 %all-gather.3.cloned.1.call-start = ((), (), s32[]{:S(2)}) async-start(), calls=%async_computation | async-start | bytes 14155776 | tf_op jit(solution)/shard_map/all_gather | solution.py:232
  7.3 216.7 %all-gather.5.cloned.1.call-start = ((), (), s32[]{:S(2)}) async-start(), calls=%async_computation.1 | async-start | bytes 9437184 | tf_op jit(solution)/shard_map/all_gather | solution.py:233
  131.3 18.1 %collective-permute-start = (bf16[128,512]{1,0:T(8,128)(2,1)}, bf16[128,512]{1,0:T(8,128)(2,1)S(1)}, u32[]{:S(2)}, u32[]{:S(2)}) collective-permute-start(bf16[128,512]{1,0:T(8,128)(2,1)} %get-tuple-element.27), channel_id=1, source_target_pairs={{0,4},{1,5},{2,6},{3,7},{4,0},{5,1},{6,2},{7,3},{8,12},{9,13},{10,... | collective-permute-start | bytes 393224 | tf_op jit(solution)/shard_map/ppermute | solution.py:24
  132.5 25.3 %collective-permute-start.3 = (bf16[128,512]{1,0:T(8,128)(2,1)}, bf16[128,512]{1,0:T(8,128)(2,1)S(1)}, u32[]{:S(2)}, u32[]{:S(2)}) collective-permute-start(bf16[128,512]{1,0:T(8,128)(2,1)} %get-tuple-element.28), channel_id=1, source_target_pairs={{0,4},{1,5},{2,6},{3,7},{4,0},{5,1},{6,2},{7,3},{8,12},{9,13},{10,... | collective-permute-start | bytes 393224 | tf_op jit(solution)/shard_map/ppermute | solution.py:24
  150.3 36.1 %collective-permute-start.1 = (bf16[256,512]{1,0:T(8,128)(2,1)S(1)}, bf16[256,512]{1,0:T(8,128)(2,1)S(1)}, u32[]{:S(2)}, u32[]{:S(2)}) collective-permute-start(bf16[256,512]{1,0:T(8,128)(2,1)S(1)} %pad_maximum_fusion.2), channel_id=1, source_target_pairs={{0,2},{1,3},{2,0},{3,1},{4,6},{5,7},{6,4},{7,5},{8,10},{9,11},{10,... | collective-permute-start | bytes 786440 | tf_op jit(solution)/shard_map/ppermute | solution.py:24
  158.8 49.0 %collective-permute-start.4 = (bf16[256,512]{1,0:T(8,128)(2,1)S(1)}, bf16[256,512]{1,0:T(8,128)(2,1)S(1)}, u32[]{:S(2)}, u32[]{:S(2)}) collective-permute-start(bf16[256,512]{1,0:T(8,128)(2,1)S(1)} %pad_maximum_fusion.3), channel_id=1, source_target_pairs={{0,2},{1,3},{2,0},{3,1},{4,6},{5,7},{6,4},{7,5},{8,10},{9,11},{10,... | collective-permute-start | bytes 786440 | tf_op jit(solution)/shard_map/ppermute | solution.py:24
  186.4 37.6 %collective-permute-start.2 = (bf16[512,512]{1,0:T(8,128)(2,1)S(1)}, bf16[512,512]{1,0:T(8,128)(2,1)}, u32[]{:S(2)}, u32[]{:S(2)}) collective-permute-start(bf16[512,512]{1,0:T(8,128)(2,1)S(1)} %constant_dynamic-update-slice_fusion.refs_0_), channel_id=1, source_target_pairs={{0,1},{1,0},{2,3},{3,2},{4,5},{5,4},{6,7},{7,6},{8,9},{9,8},{10,11... | collective-permute-start | bytes 1572872 | tf_op jit(solution)/shard_map/ppermute | solution.py:24
  207.8 16.2 %collective-permute-start.5 = (bf16[512,512]{1,0:T(8,128)(2,1)S(1)}, bf16[512,512]{1,0:T(8,128)(2,1)}, u32[]{:S(2)}, u32[]{:S(2)}) collective-permute-start(bf16[512,512]{1,0:T(8,128)(2,1)S(1)} %constant_dynamic-update-slice_fusion.3.refs_2_), channel_id=1, source_target_pairs={{0,1},{1,0},{2,3},{3,2},{4,5},{5,4},{6,7},{7,6},{8,9},{9,8},{10,11... | collective-permute-start | bytes 1572872 | tf_op jit(solution)/shard_map/ppermute | solution.py:24
  234.9 15.3 %collective-permute-start.6 = (bf16[128,2048]{1,0:T(8,128)(2,1)}, bf16[128,2048]{1,0:T(8,128)(2,1)S(1)}, u32[]{:S(2)}, u32[]{:S(2)}) collective-permute-start(bf16[128,2048]{1,0:T(8,128)(2,1)} %attend_out.7), channel_id=1, source_target_pairs={{0,8},{8,16},{16,24},{1,9},{9,17},{17,25},{2,10},{10,18},{18,26},{... | collective-permute-start | bytes 1572872 | tf_op jit(solution)/shard_map/ppermute | solution.py:253
  255.0 11.0 %collective-permute-start.7 = (bf16[128,512]{1,0:T(8,128)(2,1)}, bf16[128,512]{1,0:T(8,128)(2,1)S(1)}, u32[]{:S(2)}, u32[]{:S(2)}) collective-permute-start(bf16[128,512]{1,0:T(8,128)(2,1)} %get-tuple-element.30), channel_id=1, source_target_pairs={{0,4},{1,5},{2,6},{3,7},{4,0},{5,1},{6,2},{7,3},{8,12},{9,13},{10,... | collective-permute-start | bytes 393224 | tf_op jit(solution)/shard_map/ppermute | solution.py:24
  256.0 12.9 %collective-permute-start.10 = (bf16[128,512]{1,0:T(8,128)(2,1)}, bf16[128,512]{1,0:T(8,128)(2,1)S(1)}, u32[]{:S(2)}, u32[]{:S(2)}) collective-permute-start(bf16[128,512]{1,0:T(8,128)(2,1)} %get-tuple-element.31), channel_id=1, source_target_pairs={{0,4},{1,5},{2,6},{3,7},{4,0},{5,1},{6,2},{7,3},{8,12},{9,13},{10,... | collective-permute-start | bytes 393224 | tf_op jit(solution)/shard_map/ppermute | solution.py:24
  274.2 13.3 %collective-permute-start.9 = (bf16[512,512]{1,0:T(8,128)(2,1)S(1)}, bf16[512,512]{1,0:T(8,128)(2,1)}, u32[]{:S(2)}, u32[]{:S(2)}) collective-permute-start(bf16[512,512]{1,0:T(8,128)(2,1)S(1)} %constant_dynamic-update-slice_fusion.22.refs_0_), channel_id=1, source_target_pairs={{0,1},{1,0},{2,3},{3,2},{4,5},{5,4},{6,7},{7,6},{8,9},{9,8},{10,11... | collective-permute-start | bytes 1572872 | tf_op jit(solution)/shard_map/ppermute | solution.py:24
  298.5 15.4 %collective-permute-start.13 = (bf16[128,2048]{1,0:T(8,128)(2,1)}, bf16[128,2048]{1,0:T(8,128)(2,1)S(1)}, u32[]{:S(2)}, u32[]{:S(2)}) collective-permute-start(bf16[128,2048]{1,0:T(8,128)(2,1)} %attend_out.8), channel_id=1, source_target_pairs={{0,8},{8,16},{16,24},{1,9},{9,17},{17,25},{2,10},{10,18},{18,26},{... | collective-permute-start | bytes 1572872 | tf_op jit(solution)/shard_map/ppermute | solution.py:253
  318.7 11.9 %collective-permute-start.14 = (bf16[128,512]{1,0:T(8,128)(2,1)}, bf16[128,512]{1,0:T(8,128)(2,1)S(1)}, u32[]{:S(2)}, u32[]{:S(2)}) collective-permute-start(bf16[128,512]{1,0:T(8,128)(2,1)} %get-tuple-element.33), channel_id=1, source_target_pairs={{0,4},{1,5},{2,6},{3,7},{4,0},{5,1},{6,2},{7,3},{8,12},{9,13},{10,... | collective-permute-start | bytes 393224 | tf_op jit(solution)/shard_map/ppermute | solution.py:24
  320.5 12.9 %collective-permute-start.17 = (bf16[128,512]{1,0:T(8,128)(2,1)}, bf16[128,512]{1,0:T(8,128)(2,1)S(1)}, u32[]{:S(2)}, u32[]{:S(2)}) collective-permute-start(bf16[128,512]{1,0:T(8,128)(2,1)} %get-tuple-element.34), channel_id=1, source_target_pairs={{0,4},{1,5},{2,6},{3,7},{4,0},{5,1},{6,2},{7,3},{8,12},{9,13},{10,... | collective-permute-start | bytes 393224 | tf_op jit(solution)/shard_map/ppermute | solution.py:24
  338.9 13.2 %collective-permute-start.16 = (bf16[512,512]{1,0:T(8,128)(2,1)S(1)}, bf16[512,512]{1,0:T(8,128)(2,1)}, u32[]{:S(2)}, u32[]{:S(2)}) collective-permute-start(bf16[512,512]{1,0:T(8,128)(2,1)S(1)} %constant_dynamic-update-slice_fusion.28.refs_0_), channel_id=1, source_target_pairs={{0,1},{1,0},{2,3},{3,2},{4,5},{5,4},{6,7},{7,6},{8,9},{9,8},{10,11... | collective-permute-start | bytes 1572872 | tf_op jit(solution)/shard_map/ppermute | solution.py:24
  363.0 16.4 %collective-permute-start.20 = (bf16[128,2048]{1,0:T(8,128)(2,1)}, bf16[128,2048]{1,0:T(8,128)(2,1)S(1)}, u32[]{:S(2)}, u32[]{:S(2)}) collective-permute-start(bf16[128,2048]{1,0:T(8,128)(2,1)} %attend_out.9), channel_id=1, source_target_pairs={{0,8},{8,16},{16,24},{1,9},{9,17},{17,25},{2,10},{10,18},{18,26},{... | collective-permute-start | bytes 1572872 | tf_op jit(solution)/shard_map/ppermute | solution.py:253
  384.2 11.9 %collective-permute-start.21 = (bf16[128,512]{1,0:T(8,128)(2,1)}, bf16[128,512]{1,0:T(8,128)(2,1)S(1)}, u32[]{:S(2)}, u32[]{:S(2)}) collective-permute-start(bf16[128,512]{1,0:T(8,128)(2,1)} %get-tuple-element.36), channel_id=1, source_target_pairs={{0,4},{1,5},{2,6},{3,7},{4,0},{5,1},{6,2},{7,3},{8,12},{9,13},{10,... | collective-permute-start | bytes 393224 | tf_op jit(solution)/shard_map/ppermute | solution.py:24
  385.9 12.9 %collective-permute-start.24 = (bf16[128,512]{1,0:T(8,128)(2,1)}, bf16[128,512]{1,0:T(8,128)(2,1)S(1)}, u32[]{:S(2)}, u32[]{:S(2)}) collective-permute-start(bf16[128,512]{1,0:T(8,128)(2,1)} %get-tuple-element.37), channel_id=1, source_target_pairs={{0,4},{1,5},{2,6},{3,7},{4,0},{5,1},{6,2},{7,3},{8,12},{9,13},{10,... | collective-permute-start | bytes 393224 | tf_op jit(solution)/shard_map/ppermute | solution.py:24
  404.3 13.2 %collective-permute-start.23 = (bf16[512,512]{1,0:T(8,128)(2,1)S(1)}, bf16[512,512]{1,0:T(8,128)(2,1)S(1)}, u32[]{:S(2)}, u32[]{:S(2)}) collective-permute-start(bf16[512,512]{1,0:T(8,128)(2,1)S(1)} %constant_dynamic-update-slice_fusion.34.refs_0_), channel_id=1, source_target_pairs={{0,1},{1,0},{2,3},{3,2},{4,5},{5,4},{6,7},{7,6},{8,9},{9,8},{10,11... | collective-permute-start | bytes 1572872 | tf_op jit(solution)/shard_map/ppermute | solution.py:24
  430.0 16.4 %collective-permute-start.27 = (bf16[128,2048]{1,0:T(8,128)(2,1)}, bf16[128,2048]{1,0:T(8,128)(2,1)S(1)}, u32[]{:S(2)}, u32[]{:S(2)}) collective-permute-start(bf16[128,2048]{1,0:T(8,128)(2,1)} %attend_out.10), channel_id=1, source_target_pairs={{0,8},{8,16},{16,24},{1,9},{9,17},{17,25},{2,10},{10,18},{18,26},{... | collective-permute-start | bytes 1572872 | tf_op jit(solution)/shard_map/ppermute | solution.py:253
  451.1 11.9 %collective-permute-start.28 = (bf16[128,512]{1,0:T(8,128)(2,1)}, bf16[128,512]{1,0:T(8,128)(2,1)S(1)}, u32[]{:S(2)}, u32[]{:S(2)}) collective-permute-start(bf16[128,512]{1,0:T(8,128)(2,1)} %get-tuple-element.39), channel_id=1, source_target_pairs={{0,4},{1,5},{2,6},{3,7},{4,0},{5,1},{6,2},{7,3},{8,12},{9,13},{10,... | collective-permute-start | bytes 393224 | tf_op jit(solution)/shard_map/ppermute | solution.py:24
  452.9 12.9 %collective-permute-start.31 = (bf16[128,512]{1,0:T(8,128)(2,1)}, bf16[128,512]{1,0:T(8,128)(2,1)S(1)}, u32[]{:S(2)}, u32[]{:S(2)}) collective-permute-start(bf16[128,512]{1,0:T(8,128)(2,1)} %get-tuple-element.40), channel_id=1, source_target_pairs={{0,4},{1,5},{2,6},{3,7},{4,0},{5,1},{6,2},{7,3},{8,12},{9,13},{10,... | collective-permute-start | bytes 393224 | tf_op jit(solution)/shard_map/ppermute | solution.py:24
  471.3 13.2 %collective-permute-start.30 = (bf16[512,512]{1,0:T(8,128)(2,1)S(1)}, bf16[512,512]{1,0:T(8,128)(2,1)S(1)}, u32[]{:S(2)}, u32[]{:S(2)}) collective-permute-start(bf16[512,512]{1,0:T(8,128)(2,1)S(1)} %constant_dynamic-update-slice_fusion.40.refs_0_), channel_id=1, source_target_pairs={{0,1},{1,0},{2,3},{3,2},{4,5},{5,4},{6,7},{7,6},{8,9},{9,8},{10,11... | collective-permute-start | bytes 1572872 | tf_op jit(solution)/shard_map/ppermute | solution.py:24
  497.0 16.5 %collective-permute-start.34 = (bf16[128,2048]{1,0:T(8,128)(2,1)}, bf16[128,2048]{1,0:T(8,128)(2,1)S(1)}, u32[]{:S(2)}, u32[]{:S(2)}) collective-permute-start(bf16[128,2048]{1,0:T(8,128)(2,1)} %attend_out.11), channel_id=1, source_target_pairs={{0,8},{8,16},{16,24},{1,9},{9,17},{17,25},{2,10},{10,18},{18,26},{... | collective-permute-start | bytes 1572872 | tf_op jit(solution)/shard_map/ppermute | solution.py:253
  518.3 11.9 %collective-permute-start.35 = (bf16[128,512]{1,0:T(8,128)(2,1)}, bf16[128,512]{1,0:T(8,128)(2,1)S(1)}, u32[]{:S(2)}, u32[]{:S(2)}) collective-permute-start(bf16[128,512]{1,0:T(8,128)(2,1)} %get-tuple-element.42), channel_id=1, source_target_pairs={{0,4},{1,5},{2,6},{3,7},{4,0},{5,1},{6,2},{7,3},{8,12},{9,13},{10,... | collective-permute-start | bytes 393224 | tf_op jit(solution)/shard_map/ppermute | solution.py:24
  520.0 13.0 %collective-permute-start.38 = (bf16[128,512]{1,0:T(8,128)(2,1)}, bf16[128,512]{1,0:T(8,128)(2,1)S(1)}, u32[]{:S(2)}, u32[]{:S(2)}) collective-permute-start(bf16[128,512]{1,0:T(8,128)(2,1)} %get-tuple-element.43), channel_id=1, source_target_pairs={{0,4},{1,5},{2,6},{3,7},{4,0},{5,1},{6,2},{7,3},{8,12},{9,13},{10,... | collective-permute-start | bytes 393224 | tf_op jit(solution)/shard_map/ppermute | solution.py:24
  538.4 13.9 %collective-permute-start.37 = (bf16[512,512]{1,0:T(8,128)(2,1)S(1)}, bf16[512,512]{1,0:T(8,128)(2,1)}, u32[]{:S(2)}, u32[]{:S(2)}) collective-permute-start(bf16[512,512]{1,0:T(8,128)(2,1)S(1)} %constant_dynamic-update-slice_fusion.46.refs_0_), channel_id=1, source_target_pairs={{0,1},{1,0},{2,3},{3,2},{4,5},{5,4},{6,7},{7,6},{8,9},{9,8},{10,11... | collective-permute-start | bytes 1572872 | tf_op jit(solution)/shard_map/ppermute | solution.py:24
  563.4 16.5 %collective-permute-start.41 = (bf16[128,2048]{1,0:T(8,128)(2,1)}, bf16[128,2048]{1,0:T(8,128)(2,1)S(1)}, u32[]{:S(2)}, u32[]{:S(2)}) collective-permute-start(bf16[128,2048]{1,0:T(8,128)(2,1)} %attend_out.12), channel_id=1, source_target_pairs={{0,8},{8,16},{16,24},{1,9},{9,17},{17,25},{2,10},{10,18},{18,26},{... | collective-permute-start | bytes 1572872 | tf_op jit(solution)/shard_map/ppermute | solution.py:253
  584.7 11.9 %collective-permute-start.42 = (bf16[128,512]{1,0:T(8,128)(2,1)}, bf16[128,512]{1,0:T(8,128)(2,1)S(1)}, u32[]{:S(2)}, u32[]{:S(2)}) collective-permute-start(bf16[128,512]{1,0:T(8,128)(2,1)} %get-tuple-element.45), channel_id=1, source_target_pairs={{0,4},{1,5},{2,6},{3,7},{4,0},{5,1},{6,2},{7,3},{8,12},{9,13},{10,... | collective-permute-start | bytes 393224 | tf_op jit(solution)/shard_map/ppermute | solution.py:24
  586.4 13.0 %collective-permute-start.45 = (bf16[128,512]{1,0:T(8,128)(2,1)}, bf16[128,512]{1,0:T(8,128)(2,1)S(1)}, u32[]{:S(2)}, u32[]{:S(2)}) collective-permute-start(bf16[128,512]{1,0:T(8,128)(2,1)} %get-tuple-element.46), channel_id=1, source_target_pairs={{0,4},{1,5},{2,6},{3,7},{4,0},{5,1},{6,2},{7,3},{8,12},{9,13},{10,... | collective-permute-start | bytes 393224 | tf_op jit(solution)/shard_map/ppermute | solution.py:24
  604.9 14.6 %collective-permute-start.44 = (bf16[512,512]{1,0:T(8,128)(2,1)S(1)}, bf16[512,512]{1,0:T(8,128)(2,1)}, u32[]{:S(2)}, u32[]{:S(2)}) collective-permute-start(bf16[512,512]{1,0:T(8,128)(2,1)S(1)} %constant_dynamic-update-slice_fusion.52.refs_0_), channel_id=1, source_target_pairs={{0,1},{1,0},{2,3},{3,2},{4,5},{5,4},{6,7},{7,6},{8,9},{9,8},{10,11... | collective-permute-start | bytes 1572872 | tf_op jit(solution)/shard_map/ppermute | solution.py:24
  (48 other events, 414.8 us)
Sparse Core Ops, SparseCore 0:
  9.0 118.2 all-gather.2
  128.9 95.0 all-gather.4

commit v2 on v1

--- a/solution.py
+++ b/solution.py
@@ -32,8 +32,9 @@
     return jnp.concatenate(heads, axis=1)
 
 
-def kv_kernel(mi_ref, hidden_ref, gain_ref, w_ref, cos_ref, sin_ref, key_ref, value_ref, normed_ref):
+def kv_kernel(mi_ref, hidden_ref, gain_ref, w_ref, cos_ref, sin_ref, piece_ref, normed_ref):
     step = pl.program_id(0)
+    rows = cos_ref.shape[1]
 
     @pl.when(step == 0)
     def _():
@@ -45,11 +46,11 @@
 
     @pl.when(step == 0)
     def _():
-        key_ref[...] = rotate_heads(projected, cos_ref[0], sin_ref[0]).astype(jnp.bfloat16)
+        piece_ref[:rows, :] = rotate_heads(projected, cos_ref[0], sin_ref[0]).astype(jnp.bfloat16)
 
     @pl.when(step == 1)
     def _():
-        value_ref[...] = projected.astype(jnp.bfloat16)
+        piece_ref[rows:, :] = projected.astype(jnp.bfloat16)
 
 
 def query_kernel(mi_ref, normed_ref, w_ref, cos_ref, sin_ref, query_ref):
@@ -57,12 +58,9 @@
     query_ref[...] = rotate_heads(projected, cos_ref[0], sin_ref[0]).astype(jnp.bfloat16)
 
 
-def back_kernel(
-    mi_ref, query_ref, *refs
-):
-    count = (len(refs) - 9) // 2
-    key_refs, value_refs = refs[:count], refs[count : 2 * count]
-    qcode_ref, qpos_ref, kcode_ref, kpos_ref, hidden_ref, w_ref, out_ref, acc_ref, bias_ref = refs[2 * count :]
+def back_kernel(mi_ref, query_ref, *refs):
+    piece_refs = refs[:-9]
+    qcode_ref, qpos_ref, kcode_ref, kpos_ref, hidden_ref, w_ref, out_ref, acc_ref, bias_ref = refs[-9:]
     step = pl.program_id(0)
 
     @pl.when(step == 0)
@@ -71,25 +69,27 @@
         bias_ref[...] = jnp.where(visible, 0.0, -1e30).astype(jnp.float32)
         acc_ref[...] = hidden_ref[...].astype(jnp.float32)
 
-    part = key_refs[0].shape[0]
+    rows = query_ref.shape[0]
+    part = piece_refs[0].shape[0] // 2
     factor = HEAD_DIM ** (-0.5) * math.log2(math.e)
-    heads = []
-    for g in range(GROUP):
-        query = query_ref[:, g * HEAD_DIM : (g + 1) * HEAD_DIM]
-        scores = [
-            lax.dot_general(query, ref[...], (((1,), (1,)), ((), ())), preferred_element_type=jnp.float32)
-            + bias_ref[:, i * part : (i + 1) * part]
-            for i, ref in enumerate(key_refs)
-        ]
-        row_max = functools.reduce(jnp.maximum, [jnp.max(s, axis=-1, keepdims=True) for s in scores])
-        exps = [jnp.exp2((s - row_max) * factor) for s in scores]
-        row_sum = sum(jnp.sum(e, axis=-1, keepdims=True) for e in exps)
-        combined = sum(
-            jnp.dot(e.astype(jnp.bfloat16), ref[...], preferred_element_type=jnp.float32)
-            for e, ref in zip(exps, value_refs)
-        )
-        heads.append((combined / row_sum).astype(jnp.bfloat16))
-    attended = jnp.concatenate(heads, axis=1)
+    query = jnp.concatenate([query_ref[:, g * HEAD_DIM : (g + 1) * HEAD_DIM] for g in range(GROUP)], axis=0)
+    scores = [
+        lax.dot_general(query, ref[:part, :], (((1,), (1,)), ((), ())), preferred_element_type=jnp.float32)
+        + jnp.concatenate([bias_ref[:, i * part : (i + 1) * part]] * GROUP, axis=0)
+        for i, ref in enumerate(piece_refs)
+    ]
+    row_max = jnp.max(functools.reduce(jnp.maximum, scores), axis=-1, keepdims=True)
+    exps = [jnp.exp2((s - row_max) * factor) for s in scores]
+    row_sum = jnp.sum(functools.reduce(jnp.add, exps), axis=-1, keepdims=True)
+    combined = functools.reduce(
+        jnp.add,
+        [
+            jnp.dot(e.astype(jnp.bfloat16), ref[part:, :], preferred_element_type=jnp.float32)
+            for e, ref in zip(exps, piece_refs)
+        ],
+    )
+    heads = (combined / row_sum).astype(jnp.bfloat16)
+    attended = jnp.concatenate([heads[g * rows : (g + 1) * rows] for g in range(GROUP)], axis=1)
     acc_ref[...] += jnp.dot(attended, w_ref[...], preferred_element_type=jnp.float32)
 
     @pl.when(step == KV_HEADS - 1)
@@ -133,10 +133,9 @@
             micro_spec((rows, HEAD_DIM)),
             micro_spec((rows, HEAD_DIM)),
         ],
-        [whole_spec((rows, KEY_COLS)), whole_spec((rows, KEY_COLS)), whole_spec((rows, width))],
-        [
-            jax.ShapeDtypeStruct((rows, KEY_COLS), jnp.bfloat16),
-            jax.ShapeDtypeStruct((rows, KEY_COLS), jnp.bfloat16),
+        [whole_spec((2 * rows, KEY_COLS)), whole_spec((rows, width))],
+        [
+            jax.ShapeDtypeStruct((2 * rows, KEY_COLS), jnp.bfloat16),
             jax.ShapeDtypeStruct((rows, width), jnp.bfloat16),
         ],
         name="project_kv",
@@ -161,17 +160,15 @@
     )(mi, normed, weight, cosine, sine)
 
 
-def attend_out(mi, query, keys, values, tables, hidden, weight):
+def attend_out(mi, query, pieces, tables, hidden, weight):
     rows, width = hidden.shape
     cols = GROUP * HEAD_DIM
-    key_rows = sum(k.shape[0] for k in keys)
-    kv_specs = [pl.BlockSpec((k.shape[0], HEAD_DIM), lambda j, mi: (0, j)) for k in keys]
+    key_rows = sum(p.shape[0] for p in pieces) // 2
     return call(
         back_kernel,
         KV_HEADS,
         [pl.BlockSpec((rows, cols), lambda j, mi: (0, j))]
-        + kv_specs
-        + kv_specs
+        + [pl.BlockSpec((p.shape[0], HEAD_DIM), lambda j, mi: (0, j)) for p in pieces]
         + [
             micro_spec((rows, 1)),
             micro_spec((rows, 1)),
@@ -184,14 +181,19 @@
         jax.ShapeDtypeStruct((rows, width), jnp.bfloat16),
         scratch=[pltpu.VMEM((rows, width), jnp.float32), pltpu.VMEM((rows, key_rows), jnp.float32)],
         name="attend_out",
-    )(mi, query, *keys, *values, *tables, hidden, weight)
-
-
-def collect(own):
-    block = own
-    for bit in reversed(range(1, CYCLE_MAX.bit_length() - 1)):
-        block = jnp.concatenate([block, swapped(block, bit)], axis=0)
-    return [block, swapped(block, 0)]
+    )(mi, query, *pieces, *tables, hidden, weight)
+
+
+def collect(own, make_query):
+    pieces = [own]
+    query = None
+    for bit in reversed(range(CYCLE_MAX.bit_length() - 1)):
+        arrived = [swapped(piece, bit) for piece in pieces]
+        if query is None:
+            query = make_query()
+            arrived[0], query = lax.optimization_barrier((arrived[0], query))
+        pieces = pieces + arrived
+    return pieces, query
 
 
 def key_order():
@@ -234,6 +236,7 @@
 
     outputs = jnp.zeros((micro_count, tok_rows, model_width), jnp.bfloat16)
     carried = None
+    ahead = [(i, i + 1) for i in range(sections - 1)]
     turn_count = micro_count + sections - 1
     for turn in range(turn_count):
         offset = turn - section_index
@@ -245,12 +248,11 @@
             hidden = jnp.where(section_index == 0, x_in[turn], carried)
         else:
             hidden = carried
-        key_own, value_own, normed = project_kv(mi, hidden, norm_gain, qkv_full, cosine, sine)
-        keys, values = collect(key_own), collect(value_own)
-        query = project_query(mi, normed, qkv_full, cosine, sine)
-        result = attend_out(mi, query, keys, values, tables, hidden, out_full)
+        own, normed = project_kv(mi, hidden, norm_gain, qkv_full, cosine, sine)
+        pieces, query = collect(own, lambda: project_query(mi, normed, qkv_full, cosine, sine))
+        result = attend_out(mi, query, pieces, tables, hidden, out_full)
         if turn + 1 < turn_count:
-            carried = lax.ppermute(result, "pp", [(i, i + 1) for i in range(sections - 1)])
+            carried = lax.ppermute(result, "pp", ahead)
         kept = result
         if turn >= micro_count:
             kept = jnp.where(offset < micro_count, result, outputs[micro_count - 1])

time: 641 us -> 588 us (0.917)
  starting transfers between devices: 53.3 us -> 33.5 us
  waiting for transfers between devices: 377 us -> 364 us
  other arithmetic: 20.8 us -> 7.96 us
  local copies, waits for them, and re-layouts: 27.2 us -> 17.3 us
    ppermute x42 -> x49, waiting for transfers between devices: 167 us -> 130 us  [swapped(): lax.ppermute(array, 'cp', [(i, i ^ 1 << bit) for i in range(lax.axis_size...]
    all_gather x1, waiting for transfers between devices: 7.7 us -> 31.3 us  [body(): out_full = lax.all_gather(w_out, 'cp', axis=1, tiled=True)[0]]
    ppermute x42 -> x49, starting transfers between devices: 45 us -> 25.3 us  [swapped(): lax.ppermute(array, 'cp', [(i, i ^ 1 << bit) for i in range(lax.axis_size...]
    concatenate x14 -> x0, other arithmetic: 12.9 us -> none  [collect(): block = jnp.concatenate([block, swapped(block, bit)], axis=0)]
    unnamed x102 -> x130, local copies, waits for them, and re-layouts: 21.9 us -> 12 us
  transfers between devices with their start and end apart: 50 -> 57, of which waited for: 36 -> 24; matrix products, arithmetic and copies ran while one was open for 6% -> 2% of each run, Pallas kernels for 7% -> 8%
where the time goes in v2:
time: 588 us; the launch traced here: 587 us
  waiting for transfers between devices  364 us (62%)
  Pallas kernels  150 us (26%)
  starting transfers between devices  33.5 us (6%)
  local copies, waits for them, and re-layouts  17.3 us (3%)
  between operations  14.1 us (2%)
  other arithmetic  7.96 us (1%)
    ppermute x49, waiting for transfers between devices, swapped(): lax.ppermute(array, 'cp', [(i, i ^ 1 << bit) for i in range(lax.axis_size...  130 us
    all_gather x1, waiting for transfers between devices, body(): qkv_full = lax.all_gather(w_qkv, 'cp', axis=1, tiled=True)[0]  115 us
    ppermute x6, waiting for transfers between devices, body(): carried = lax.ppermute(result, 'pp', ahead)  86.3 us
    pallas_call x7, Pallas kernels, attend_out(): call(back_kernel, KV_HEADS, [pl.BlockSpec((rows, cols), lambda j, mi: (0,...  80 us
    pallas_call x7, Pallas kernels, project_query(): call(query_kernel, 4, [whole_spec((rows, width)), pl.BlockSpec((width, co...  42.9 us
    all_gather x1, waiting for transfers between devices, body(): out_full = lax.all_gather(w_out, 'cp', axis=1, tiled=True)[0]  31.3 us
    pallas_call x7, Pallas kernels, project_kv(): call(kv_kernel, 2, [whole_spec((rows, width)), whole_spec((1, width)), pl...  27.5 us
    ppermute x49, starting transfers between devices, swapped(): lax.ppermute(array, 'cp', [(i, i ^ 1 << bit) for i in range(lax.axis_size...  25.3 us
  transfers between devices with their start and end apart: 57, of which 24 were waited for; matrix products, arithmetic and copies ran while one was open for 2% of the time, Pallas kernels for 8%

profile of v2, /device:TPU:7, one launch (start us, length us, event | category | flops | bytes accessed | tf_op | source)
XLA Modules:
  0.0 587.1 jit_solution(1794963091420768006)
XLA Ops:
  12.4 114.9 %all-gather.3.cloned.1.call-done = bf16[1,2048,3072]{2,1,0:T(8,128)(2,1)} async-done(((bf16[1,256,3072]{2,1,0:T(8,128)(2,1)}), bf16[1,2048,3072]{2,1,0:T(8,128)(2,1)}) %all-gather.3.cloned.1.call-update) | async-done | bytes 12582928 | tf_op jit(solution)/shard_map/all_gather | solution.py:234
  131.8 6.4 %project_query.7.query_ref = bf16[128,2048]{1,0:T(8,128)(2,1)} custom-call(s32[1]{0:T(128)} %bitcast.mi_ref, bf16[128,2048]{1,0:T(8,128)(2,1)} %get-tuple-element.34.normed_ref, bf16[2048,3072]{1,0:T(8,128)(2,1)} %bitcast.130, f32[4,128,128]{2,1,0:T(8,128)} %pad_maximum_fusion.cos_ref, f32[4,128,128]{2,1,0:T(8,128)} %pad_maximum_fusion.1.sin_ref), custom_call_target="tpu_custom_call" | custom-call | tf_op jit(solution)/shard_map/project_query/pallas_call | solution.py:148
  138.2 16.7 %collective-permute-done.refs_1_ = bf16[256,512]{1,0:T(8,128)(2,1)S(1)} collective-permute-done((bf16[256,512]{1,0:T(8,128)(2,1)}, bf16[256,512]{1,0:T(8,128)(2,1)S(1)}, u32[]{:S(2)}, u32[]{:S(2)}) %collective-permute-start) | collective-permute-done | bytes 262176 | tf_op jit(solution)/shard_map/ppermute | solution.py:24
  156.1 29.5 %collective-permute-done.2.refs_3_ = bf16[256,512]{1,0:T(8,128)(2,1)S(1)} collective-permute-done((bf16[256,512]{1,0:T(8,128)(2,1)S(1)}, bf16[256,512]{1,0:T(8,128)(2,1)S(1)}, u32[]{:S(2)}, u32[]{:S(2)}) %collective-permute-start.2) | collective-permute-done | bytes 262176 | tf_op jit(solution)/shard_map/ppermute | solution.py:24
  189.4 31.3 %all-gather.5.cloned.1.call-done = bf16[1,2048,2048]{2,1,0:T(8,128)(2,1)} async-done(((bf16[1,256,2048]{2,1,0:T(8,128)(2,1)}), bf16[1,2048,2048]{2,1,0:T(8,128)(2,1)}) %all-gather.5.cloned.1.call-update) | async-done | bytes 8388624 | tf_op jit(solution)/shard_map/all_gather | solution.py:235
  221.4 11.4 %attend_out.7 = bf16[128,2048]{1,0:T(8,128)(2,1)} custom-call(s32[1]{0:T(128)} %bitcast.mi_ref, bf16[128,2048]{1,0:T(8,128)(2,1)} %project_query.7.query_ref, bf16[256,512]{1,0:T(8,128)(2,1)} %get-tuple-element.33.refs_0_, bf16[256,512]{1,0:T(8,128)(2,1)} %copy-done.10, bf16[256,512]{1,0:T(8,128)(2,1)} %copy-done.11, bf16[256,512]{1,0:T(8,128)(2,1)} %copy-done.15, ...), custom_call_target="tpu_custom_call" | custom-call | tf_op jit(solution)/shard_map/attend_out/pallas_call | solution.py:167
  234.2 14.0 %collective-permute-done.7 = bf16[128,2048]{1,0:T(8,128)(2,1)S(1)} collective-permute-done((bf16[128,2048]{1,0:T(8,128)(2,1)}, bf16[128,2048]{1,0:T(8,128)(2,1)S(1)}, u32[]{:S(2)}, u32[]{:S(2)}) %collective-permute-start.7) | collective-permute-done | bytes 524320 | tf_op jit(solution)/shard_map/ppermute | solution.py:255
  260.1 7.7 %collective-permute-done.8.refs_1_ = bf16[256,512]{1,0:T(8,128)(2,1)S(1)} collective-permute-done((bf16[256,512]{1,0:T(8,128)(2,1)}, bf16[256,512]{1,0:T(8,128)(2,1)S(1)}, u32[]{:S(2)}, u32[]{:S(2)}) %collective-permute-start.8) | collective-permute-done | bytes 262176 | tf_op jit(solution)/shard_map/ppermute | solution.py:24
  268.8 6.3 %collective-permute-done.10.refs_3_ = bf16[256,512]{1,0:T(8,128)(2,1)S(1)} collective-permute-done((bf16[256,512]{1,0:T(8,128)(2,1)S(1)}, bf16[256,512]{1,0:T(8,128)(2,1)S(1)}, u32[]{:S(2)}, u32[]{:S(2)}) %collective-permute-start.10) | collective-permute-done | bytes 262176 | tf_op jit(solution)/shard_map/ppermute | solution.py:24
  278.0 11.5 %attend_out.8 = bf16[128,2048]{1,0:T(8,128)(2,1)} custom-call(s32[1]{0:T(128)} %bitcast.27.mi_ref, bf16[128,2048]{1,0:T(8,128)(2,1)} %project_query.8.query_ref, bf16[256,512]{1,0:T(8,128)(2,1)} %get-tuple-element.37.refs_0_, bf16[256,512]{1,0:T(8,128)(2,1)} %copy-done.23, bf16[256,512]{1,0:T(8,128)(2,1)} %copy-done.28, bf16[256,512]{1,0:T(8,128)(2,1)} %copy-done.35, ...), custom_call_target="tpu_custom_call" | custom-call | tf_op jit(solution)/shard_map/attend_out/pallas_call | solution.py:167
  290.9 13.9 %collective-permute-done.15 = bf16[128,2048]{1,0:T(8,128)(2,1)S(1)} collective-permute-done((bf16[128,2048]{1,0:T(8,128)(2,1)}, bf16[128,2048]{1,0:T(8,128)(2,1)S(1)}, u32[]{:S(2)}, u32[]{:S(2)}) %collective-permute-start.15) | collective-permute-done | bytes 524320 | tf_op jit(solution)/shard_map/ppermute | solution.py:255
  316.8 7.4 %collective-permute-done.16.refs_1_ = bf16[256,512]{1,0:T(8,128)(2,1)S(1)} collective-permute-done((bf16[256,512]{1,0:T(8,128)(2,1)}, bf16[256,512]{1,0:T(8,128)(2,1)S(1)}, u32[]{:S(2)}, u32[]{:S(2)}) %collective-permute-start.16) | collective-permute-done | bytes 262176 | tf_op jit(solution)/shard_map/ppermute | solution.py:24
  325.4 6.3 %collective-permute-done.18.refs_3_ = bf16[256,512]{1,0:T(8,128)(2,1)S(1)} collective-permute-done((bf16[256,512]{1,0:T(8,128)(2,1)S(1)}, bf16[256,512]{1,0:T(8,128)(2,1)S(1)}, u32[]{:S(2)}, u32[]{:S(2)}) %collective-permute-start.18) | collective-permute-done | bytes 262176 | tf_op jit(solution)/shard_map/ppermute | solution.py:24
  334.5 11.4 %attend_out.9 = bf16[128,2048]{1,0:T(8,128)(2,1)} custom-call(s32[1]{0:T(128)} %bitcast.30.mi_ref, bf16[128,2048]{1,0:T(8,128)(2,1)} %project_query.9.query_ref, bf16[256,512]{1,0:T(8,128)(2,1)} %get-tuple-element.41.refs_0_, bf16[256,512]{1,0:T(8,128)(2,1)} %copy-done.24, bf16[256,512]{1,0:T(8,128)(2,1)} %copy-done.29, bf16[256,512]{1,0:T(8,128)(2,1)} %copy-done.36, ...), custom_call_target="tpu_custom_call" | custom-call | tf_op jit(solution)/shard_map/attend_out/pallas_call | solution.py:167
  347.2 15.0 %collective-permute-done.23 = bf16[128,2048]{1,0:T(8,128)(2,1)S(1)} collective-permute-done((bf16[128,2048]{1,0:T(8,128)(2,1)}, bf16[128,2048]{1,0:T(8,128)(2,1)S(1)}, u32[]{:S(2)}, u32[]{:S(2)}) %collective-permute-start.23) | collective-permute-done | bytes 524320 | tf_op jit(solution)/shard_map/ppermute | solution.py:255
  368.5 6.1 %project_query.10.query_ref = bf16[128,2048]{1,0:T(8,128)(2,1)} custom-call(s32[1]{0:T(128)} %bitcast.33.mi_ref, bf16[128,2048]{1,0:T(8,128)(2,1)} %get-tuple-element.46.normed_ref, bf16[2048,3072]{1,0:T(8,128)(2,1)} %bitcast.136, f32[4,128,128]{2,1,0:T(8,128)} %pad_maximum_fusion.cos_ref, f32[4,128,128]{2,1,0:T(8,128)} %pad_maximum_fusion.1.sin_ref), custom_call_target="tpu_custom_call" | custom-call | tf_op jit(solution)/shard_map/project_query/pallas_call | solution.py:148
  374.5 7.2 %collective-permute-done.24.refs_1_ = bf16[256,512]{1,0:T(8,128)(2,1)S(1)} collective-permute-done((bf16[256,512]{1,0:T(8,128)(2,1)}, bf16[256,512]{1,0:T(8,128)(2,1)S(1)}, u32[]{:S(2)}, u32[]{:S(2)}) %collective-permute-start.24) | collective-permute-done | bytes 262176 | tf_op jit(solution)/shard_map/ppermute | solution.py:24
  382.8 6.3 %collective-permute-done.26.refs_3_ = bf16[256,512]{1,0:T(8,128)(2,1)S(1)} collective-permute-done((bf16[256,512]{1,0:T(8,128)(2,1)S(1)}, bf16[256,512]{1,0:T(8,128)(2,1)S(1)}, u32[]{:S(2)}, u32[]{:S(2)}) %collective-permute-start.26) | collective-permute-done | bytes 262176 | tf_op jit(solution)/shard_map/ppermute | solution.py:24
  392.3 11.4 %attend_out.10 = bf16[128,2048]{1,0:T(8,128)(2,1)} custom-call(s32[1]{0:T(128)} %bitcast.33.mi_ref, bf16[128,2048]{1,0:T(8,128)(2,1)} %project_query.10.query_ref, bf16[256,512]{1,0:T(8,128)(2,1)} %get-tuple-element.45.refs_0_, bf16[256,512]{1,0:T(8,128)(2,1)} %copy-done.25, bf16[256,512]{1,0:T(8,128)(2,1)} %copy-done.30, bf16[256,512]{1,0:T(8,128)(2,1)} %copy-done.37, ...), custom_call_target="tpu_custom_call" | custom-call | tf_op jit(solution)/shard_map/attend_out/pallas_call | solution.py:167
  405.0 14.8 %collective-permute-done.31.hidden_ref.refs_12_ = bf16[128,2048]{1,0:T(8,128)(2,1)S(1)} collective-permute-done((bf16[128,2048]{1,0:T(8,128)(2,1)}, bf16[128,2048]{1,0:T(8,128)(2,1)S(1)}, u32[]{:S(2)}, u32[]{:S(2)}) %collective-permute-start.31) | collective-permute-done | bytes 524320 | tf_op jit(solution)/shard_map/ppermute | solution.py:255
  432.2 7.1 %collective-permute-done.32.refs_1_ = bf16[256,512]{1,0:T(8,128)(2,1)S(1)} collective-permute-done((bf16[256,512]{1,0:T(8,128)(2,1)}, bf16[256,512]{1,0:T(8,128)(2,1)S(1)}, u32[]{:S(2)}, u32[]{:S(2)}) %collective-permute-start.32) | collective-permute-done | bytes 262176 | tf_op jit(solution)/shard_map/ppermute | solution.py:24
  440.4 6.3 %collective-permute-done.34.refs_3_ = bf16[256,512]{1,0:T(8,128)(2,1)S(1)} collective-permute-done((bf16[256,512]{1,0:T(8,128)(2,1)S(1)}, bf16[256,512]{1,0:T(8,128)(2,1)S(1)}, u32[]{:S(2)}, u32[]{:S(2)}) %collective-permute-start.34) | collective-permute-done | bytes 262176 | tf_op jit(solution)/shard_map/ppermute | solution.py:24
  449.9 11.5 %attend_out.11 = bf16[128,2048]{1,0:T(8,128)(2,1)} custom-call(s32[1]{0:T(128)} %bitcast.36.mi_ref, bf16[128,2048]{1,0:T(8,128)(2,1)} %project_query.11.query_ref, bf16[256,512]{1,0:T(8,128)(2,1)} %get-tuple-element.49.refs_0_, bf16[256,512]{1,0:T(8,128)(2,1)} %copy-done.26, bf16[256,512]{1,0:T(8,128)(2,1)} %copy-done.31, bf16[256,512]{1,0:T(8,128)(2,1)} %copy-done.38, ...), custom_call_target="tpu_custom_call" | custom-call | tf_op jit(solution)/shard_map/attend_out/pallas_call | solution.py:167
  462.9 14.6 %collective-permute-done.39.hidden_ref.refs_12_ = bf16[128,2048]{1,0:T(8,128)(2,1)S(1)} collective-permute-done((bf16[128,2048]{1,0:T(8,128)(2,1)}, bf16[128,2048]{1,0:T(8,128)(2,1)S(1)}, u32[]{:S(2)}, u32[]{:S(2)}) %collective-permute-start.39) | collective-permute-done | bytes 524320 | tf_op jit(solution)/shard_map/ppermute | solution.py:255
  489.8 7.2 %collective-permute-done.40.refs_1_ = bf16[256,512]{1,0:T(8,128)(2,1)} collective-permute-done((bf16[256,512]{1,0:T(8,128)(2,1)}, bf16[256,512]{1,0:T(8,128)(2,1)}, u32[]{:S(2)}, u32[]{:S(2)}) %collective-permute-start.40) | collective-permute-done | bytes 262176 | tf_op jit(solution)/shard_map/ppermute | solution.py:24
  498.0 6.7 %collective-permute-done.42.refs_3_ = bf16[256,512]{1,0:T(8,128)(2,1)} collective-permute-done((bf16[256,512]{1,0:T(8,128)(2,1)}, bf16[256,512]{1,0:T(8,128)(2,1)}, u32[]{:S(2)}, u32[]{:S(2)}) %collective-permute-start.42) | collective-permute-done | bytes 262176 | tf_op jit(solution)/shard_map/ppermute | solution.py:24
  508.5 11.4 %attend_out.12 = bf16[128,2048]{1,0:T(8,128)(2,1)} custom-call(s32[1]{0:T(128)} %bitcast.39.mi_ref, bf16[128,2048]{1,0:T(8,128)(2,1)} %project_query.12.query_ref, bf16[256,512]{1,0:T(8,128)(2,1)} %get-tuple-element.53.refs_0_, bf16[256,512]{1,0:T(8,128)(2,1)} %collective-permute-done.40.refs_1_, bf16[256,512]{1,0:T(8,128)(2,1)} %collective-permute-done.41.refs_2_, ...), custom_call_target="tpu_custom_call" | custom-call | tf_op jit(solution)/shard_map/attend_out/pallas_call | solution.py:167
  522.4 14.0 %collective-permute-done.47.hidden_ref.refs_12_ = bf16[128,2048]{1,0:T(8,128)(2,1)S(1)} collective-permute-done((bf16[128,2048]{1,0:T(8,128)(2,1)}, bf16[128,2048]{1,0:T(8,128)(2,1)S(1)}, u32[]{:S(2)}, u32[]{:S(2)}) %collective-permute-start.47) | collective-permute-done | bytes 524320 | tf_op jit(solution)/shard_map/ppermute | solution.py:255
  542.9 6.1 %project_query.13.query_ref = bf16[128,2048]{1,0:T(8,128)(2,1)} custom-call(s32[1]{0:T(128)} %bitcast.43.mi_ref, bf16[128,2048]{1,0:T(8,128)(2,1)} %get-tuple-element.58.normed_ref, bf16[2048,3072]{1,0:T(8,128)(2,1)} %bitcast.142, f32[4,128,128]{2,1,0:T(8,128)} %pad_maximum_fusion.cos_ref, f32[4,128,128]{2,1,0:T(8,128)} %pad_maximum_fusion.1.sin_ref), custom_call_target="tpu_custom_call" | custom-call | tf_op jit(solution)/shard_map/project_query/pallas_call | solution.py:148
  549.0 6.9 %collective-permute-done.48.refs_1_ = bf16[256,512]{1,0:T(8,128)(2,1)S(1)} collective-permute-done((bf16[256,512]{1,0:T(8,128)(2,1)}, bf16[256,512]{1,0:T(8,128)(2,1)S(1)}, u32[]{:S(2)}, u32[]{:S(2)}) %collective-permute-start.48) | collective-permute-done | bytes 262176 | tf_op jit(solution)/shard_map/ppermute | solution.py:24
  557.0 6.2 %collective-permute-done.50.refs_3_ = bf16[256,512]{1,0:T(8,128)(2,1)S(1)} collective-permute-done((bf16[256,512]{1,0:T(8,128)(2,1)S(1)}, bf16[256,512]{1,0:T(8,128)(2,1)S(1)}, u32[]{:S(2)}, u32[]{:S(2)}) %collective-permute-start.50) | collective-permute-done | bytes 262176 | tf_op jit(solution)/shard_map/ppermute | solution.py:24
  566.9 11.4 %attend_out.13 = bf16[128,2048]{1,0:T(8,128)(2,1)} custom-call(s32[1]{0:T(128)} %bitcast.43.mi_ref, bf16[128,2048]{1,0:T(8,128)(2,1)} %project_query.13.query_ref, bf16[256,512]{1,0:T(8,128)(2,1)} %get-tuple-element.57.refs_0_, bf16[256,512]{1,0:T(8,128)(2,1)} %copy-done.13, bf16[256,512]{1,0:T(8,128)(2,1)} %copy-done.16, bf16[256,512]{1,0:T(8,128)(2,1)} %copy-done.18, ...), custom_call_target="tpu_custom_call" | custom-call | tf_op jit(solution)/shard_map/attend_out/pallas_call | solution.py:167
  (263 shorter events, 114.3 us)
Async XLA Ops:
  6.5 120.8 %all-gather.3.cloned.1.call-start = ((), (), s32[]{:S(2)}) async-start(), calls=%async_computation | async-start | bytes 14155776 | tf_op jit(solution)/shard_map/all_gather | solution.py:234
  7.3 213.4 %all-gather.5.cloned.1.call-start = ((), (), s32[]{:S(2)}) async-start(), calls=%async_computation.1 | async-start | bytes 9437184 | tf_op jit(solution)/shard_map/all_gather | solution.py:235
  131.2 23.7 %collective-permute-start = (bf16[256,512]{1,0:T(8,128)(2,1)}, bf16[256,512]{1,0:T(8,128)(2,1)S(1)}, u32[]{:S(2)}, u32[]{:S(2)}) collective-permute-start(bf16[256,512]{1,0:T(8,128)(2,1)} %get-tuple-element.33.refs_0_), channel_id=1, source_target_pairs={{0,4},{1,5},{2,6},{3,7},{4,0},{5,1},{6,2},{7,3},{8,12},{9,13},{10,... | collective-permute-start | bytes 786440 | tf_op jit(solution)/shard_map/ppermute | solution.py:24
  131.6 24.1 %collective-permute-start.1 = (bf16[256,512]{1,0:T(8,128)(2,1)}, bf16[256,512]{1,0:T(8,128)(2,1)S(1)}, u32[]{:S(2)}, u32[]{:S(2)}) collective-permute-start(bf16[256,512]{1,0:T(8,128)(2,1)} %get-tuple-element.33.refs_0_), channel_id=1, source_target_pairs={{0,2},{1,3},{2,0},{3,1},{4,6},{5,7},{6,4},{7,5},{8,10},{9,11},{10,... | collective-permute-start | bytes 786440 | tf_op jit(solution)/shard_map/ppermute | solution.py:24
  154.9 30.6 %collective-permute-start.2 = (bf16[256,512]{1,0:T(8,128)(2,1)S(1)}, bf16[256,512]{1,0:T(8,128)(2,1)S(1)}, u32[]{:S(2)}, u32[]{:S(2)}) collective-permute-start(bf16[256,512]{1,0:T(8,128)(2,1)S(1)} %collective-permute-done.refs_1_), channel_id=1, source_target_pairs={{0,2},{1,3},{2,0},{3,1},{4,6},{5,7},{6,4},{7,5},{8,10},{9,11},{10,... | collective-permute-start | bytes 786440 | tf_op jit(solution)/shard_map/ppermute | solution.py:24
  155.0 65.7 %collective-permute-start.3 = (bf16[256,512]{1,0:T(8,128)(2,1)S(1)}, bf16[256,512]{1,0:T(8,128)(2,1)S(1)}, u32[]{:S(2)}, u32[]{:S(2)}) collective-permute-start(bf16[256,512]{1,0:T(8,128)(2,1)S(1)} %copy-done.9), channel_id=1, source_target_pairs={{0,1},{1,0},{2,3},{3,2},{4,5},{5,4},{6,7},{7,6},{8,9},{9,8},{10,11... | collective-permute-start | bytes 786440 | tf_op jit(solution)/shard_map/ppermute | solution.py:24
  155.6 65.1 %collective-permute-start.4 = (bf16[256,512]{1,0:T(8,128)(2,1)S(1)}, bf16[256,512]{1,0:T(8,128)(2,1)}, u32[]{:S(2)}, u32[]{:S(2)}) collective-permute-start(bf16[256,512]{1,0:T(8,128)(2,1)S(1)} %collective-permute-done.refs_1_), channel_id=1, source_target_pairs={{0,1},{1,0},{2,3},{3,2},{4,5},{5,4},{6,7},{7,6},{8,9},{9,8},{10,11... | collective-permute-start | bytes 786440 | tf_op jit(solution)/shard_map/ppermute | solution.py:24
  155.7 65.0 %collective-permute-start.5 = (bf16[256,512]{1,0:T(8,128)(2,1)S(1)}, bf16[256,512]{1,0:T(8,128)(2,1)}, u32[]{:S(2)}, u32[]{:S(2)}) collective-permute-start(bf16[256,512]{1,0:T(8,128)(2,1)S(1)} %collective-permute-done.1.refs_2_), channel_id=1, source_target_pairs={{0,1},{1,0},{2,3},{3,2},{4,5},{5,4},{6,7},{7,6},{8,9},{9,8},{10,11... | collective-permute-start | bytes 786440 | tf_op jit(solution)/shard_map/ppermute | solution.py:24
  185.6 35.1 %collective-permute-start.6 = (bf16[256,512]{1,0:T(8,128)(2,1)S(1)}, bf16[256,512]{1,0:T(8,128)(2,1)}, u32[]{:S(2)}, u32[]{:S(2)}) collective-permute-start(bf16[256,512]{1,0:T(8,128)(2,1)S(1)} %collective-permute-done.2.refs_3_), channel_id=1, source_target_pairs={{0,1},{1,0},{2,3},{3,2},{4,5},{5,4},{6,7},{7,6},{8,9},{9,8},{10,11... | collective-permute-start | bytes 786440 | tf_op jit(solution)/shard_map/ppermute | solution.py:24
  232.9 15.3 %collective-permute-start.7 = (bf16[128,2048]{1,0:T(8,128)(2,1)}, bf16[128,2048]{1,0:T(8,128)(2,1)S(1)}, u32[]{:S(2)}, u32[]{:S(2)}) collective-permute-start(bf16[128,2048]{1,0:T(8,128)(2,1)} %attend_out.7), channel_id=1, source_target_pairs={{0,8},{8,16},{16,24},{1,9},{9,17},{17,25},{2,10},{10,18},{18,26},{... | collective-permute-start | bytes 1572872 | tf_op jit(solution)/shard_map/ppermute | solution.py:255
  253.0 14.8 %collective-permute-start.8 = (bf16[256,512]{1,0:T(8,128)(2,1)}, bf16[256,512]{1,0:T(8,128)(2,1)S(1)}, u32[]{:S(2)}, u32[]{:S(2)}) collective-permute-start(bf16[256,512]{1,0:T(8,128)(2,1)} %get-tuple-element.37.refs_0_), channel_id=1, source_target_pairs={{0,4},{1,5},{2,6},{3,7},{4,0},{5,1},{6,2},{7,3},{8,12},{9,13},{10,... | collective-permute-start | bytes 786440 | tf_op jit(solution)/shard_map/ppermute | solution.py:24
  253.0 15.4 %collective-permute-start.9 = (bf16[256,512]{1,0:T(8,128)(2,1)}, bf16[256,512]{1,0:T(8,128)(2,1)S(1)}, u32[]{:S(2)}, u32[]{:S(2)}) collective-permute-start(bf16[256,512]{1,0:T(8,128)(2,1)} %get-tuple-element.37.refs_0_), channel_id=1, source_target_pairs={{0,2},{1,3},{2,0},{3,1},{4,6},{5,7},{6,4},{7,5},{8,10},{9,11},{10,... | collective-permute-start | bytes 786440 | tf_op jit(solution)/shard_map/ppermute | solution.py:24
  289.4 15.4 %collective-permute-start.15 = (bf16[128,2048]{1,0:T(8,128)(2,1)}, bf16[128,2048]{1,0:T(8,128)(2,1)S(1)}, u32[]{:S(2)}, u32[]{:S(2)}) collective-permute-start(bf16[128,2048]{1,0:T(8,128)(2,1)} %attend_out.8), channel_id=1, source_target_pairs={{0,8},{8,16},{16,24},{1,9},{9,17},{17,25},{2,10},{10,18},{18,26},{... | collective-permute-start | bytes 1572872 | tf_op jit(solution)/shard_map/ppermute | solution.py:255
  309.6 14.7 %collective-permute-start.16 = (bf16[256,512]{1,0:T(8,128)(2,1)}, bf16[256,512]{1,0:T(8,128)(2,1)S(1)}, u32[]{:S(2)}, u32[]{:S(2)}) collective-permute-start(bf16[256,512]{1,0:T(8,128)(2,1)} %get-tuple-element.41.refs_0_), channel_id=1, source_target_pairs={{0,4},{1,5},{2,6},{3,7},{4,0},{5,1},{6,2},{7,3},{8,12},{9,13},{10,... | collective-permute-start | bytes 786440 | tf_op jit(solution)/shard_map/ppermute | solution.py:24
  309.6 15.3 %collective-permute-start.17 = (bf16[256,512]{1,0:T(8,128)(2,1)}, bf16[256,512]{1,0:T(8,128)(2,1)S(1)}, u32[]{:S(2)}, u32[]{:S(2)}) collective-permute-start(bf16[256,512]{1,0:T(8,128)(2,1)} %get-tuple-element.41.refs_0_), channel_id=1, source_target_pairs={{0,2},{1,3},{2,0},{3,1},{4,6},{5,7},{6,4},{7,5},{8,10},{9,11},{10,... | collective-permute-start | bytes 786440 | tf_op jit(solution)/shard_map/ppermute | solution.py:24
  345.9 16.3 %collective-permute-start.23 = (bf16[128,2048]{1,0:T(8,128)(2,1)}, bf16[128,2048]{1,0:T(8,128)(2,1)S(1)}, u32[]{:S(2)}, u32[]{:S(2)}) collective-permute-start(bf16[128,2048]{1,0:T(8,128)(2,1)} %attend_out.9), channel_id=1, source_target_pairs={{0,8},{8,16},{16,24},{1,9},{9,17},{17,25},{2,10},{10,18},{18,26},{... | collective-permute-start | bytes 1572872 | tf_op jit(solution)/shard_map/ppermute | solution.py:255
  367.0 14.7 %collective-permute-start.24 = (bf16[256,512]{1,0:T(8,128)(2,1)}, bf16[256,512]{1,0:T(8,128)(2,1)S(1)}, u32[]{:S(2)}, u32[]{:S(2)}) collective-permute-start(bf16[256,512]{1,0:T(8,128)(2,1)} %get-tuple-element.45.refs_0_), channel_id=1, source_target_pairs={{0,4},{1,5},{2,6},{3,7},{4,0},{5,1},{6,2},{7,3},{8,12},{9,13},{10,... | collective-permute-start | bytes 786440 | tf_op jit(solution)/shard_map/ppermute | solution.py:24
  367.0 15.3 %collective-permute-start.25 = (bf16[256,512]{1,0:T(8,128)(2,1)}, bf16[256,512]{1,0:T(8,128)(2,1)S(1)}, u32[]{:S(2)}, u32[]{:S(2)}) collective-permute-start(bf16[256,512]{1,0:T(8,128)(2,1)} %get-tuple-element.45.refs_0_), channel_id=1, source_target_pairs={{0,2},{1,3},{2,0},{3,1},{4,6},{5,7},{6,4},{7,5},{8,10},{9,11},{10,... | collective-permute-start | bytes 786440 | tf_op jit(solution)/shard_map/ppermute | solution.py:24
  403.7 16.1 %collective-permute-start.31 = (bf16[128,2048]{1,0:T(8,128)(2,1)}, bf16[128,2048]{1,0:T(8,128)(2,1)S(1)}, u32[]{:S(2)}, u32[]{:S(2)}) collective-permute-start(bf16[128,2048]{1,0:T(8,128)(2,1)} %attend_out.10), channel_id=1, source_target_pairs={{0,8},{8,16},{16,24},{1,9},{9,17},{17,25},{2,10},{10,18},{18,26},{... | collective-permute-start | bytes 1572872 | tf_op jit(solution)/shard_map/ppermute | solution.py:255
  424.6 14.7 %collective-permute-start.32 = (bf16[256,512]{1,0:T(8,128)(2,1)}, bf16[256,512]{1,0:T(8,128)(2,1)S(1)}, u32[]{:S(2)}, u32[]{:S(2)}) collective-permute-start(bf16[256,512]{1,0:T(8,128)(2,1)} %get-tuple-element.49.refs_0_), channel_id=1, source_target_pairs={{0,4},{1,5},{2,6},{3,7},{4,0},{5,1},{6,2},{7,3},{8,12},{9,13},{10,... | collective-permute-start | bytes 786440 | tf_op jit(solution)/shard_map/ppermute | solution.py:24
  424.6 15.3 %collective-permute-start.33 = (bf16[256,512]{1,0:T(8,128)(2,1)}, bf16[256,512]{1,0:T(8,128)(2,1)S(1)}, u32[]{:S(2)}, u32[]{:S(2)}) collective-permute-start(bf16[256,512]{1,0:T(8,128)(2,1)} %get-tuple-element.49.refs_0_), channel_id=1, source_target_pairs={{0,2},{1,3},{2,0},{3,1},{4,6},{5,7},{6,4},{7,5},{8,10},{9,11},{10,... | collective-permute-start | bytes 786440 | tf_op jit(solution)/shard_map/ppermute | solution.py:24
  461.4 16.1 %collective-permute-start.39 = (bf16[128,2048]{1,0:T(8,128)(2,1)}, bf16[128,2048]{1,0:T(8,128)(2,1)S(1)}, u32[]{:S(2)}, u32[]{:S(2)}) collective-permute-start(bf16[128,2048]{1,0:T(8,128)(2,1)} %attend_out.11), channel_id=1, source_target_pairs={{0,8},{8,16},{16,24},{1,9},{9,17},{17,25},{2,10},{10,18},{18,26},{... | collective-permute-start | bytes 1572872 | tf_op jit(solution)/shard_map/ppermute | solution.py:255
  482.2 14.8 %collective-permute-start.40 = (bf16[256,512]{1,0:T(8,128)(2,1)}, bf16[256,512]{1,0:T(8,128)(2,1)}, u32[]{:S(2)}, u32[]{:S(2)}) collective-permute-start(bf16[256,512]{1,0:T(8,128)(2,1)} %get-tuple-element.53.refs_0_), channel_id=1, source_target_pairs={{0,4},{1,5},{2,6},{3,7},{4,0},{5,1},{6,2},{7,3},{8,12},{9,13},{10,... | collective-permute-start | bytes 786440 | tf_op jit(solution)/shard_map/ppermute | solution.py:24
  482.3 15.3 %collective-permute-start.41 = (bf16[256,512]{1,0:T(8,128)(2,1)}, bf16[256,512]{1,0:T(8,128)(2,1)}, u32[]{:S(2)}, u32[]{:S(2)}) collective-permute-start(bf16[256,512]{1,0:T(8,128)(2,1)} %get-tuple-element.53.refs_0_), channel_id=1, source_target_pairs={{0,2},{1,3},{2,0},{3,1},{4,6},{5,7},{6,4},{7,5},{8,10},{9,11},{10,... | collective-permute-start | bytes 786440 | tf_op jit(solution)/shard_map/ppermute | solution.py:24
  497.5 9.6 %collective-permute-start.44 = (bf16[256,512]{1,0:T(8,128)(2,1)}, bf16[256,512]{1,0:T(8,128)(2,1)S(1)}, u32[]{:S(2)}, u32[]{:S(2)}) collective-permute-start(bf16[256,512]{1,0:T(8,128)(2,1)} %collective-permute-done.40.refs_1_), channel_id=1, source_target_pairs={{0,1},{1,0},{2,3},{3,2},{4,5},{5,4},{6,7},{7,6},{8,9},{9,8},{10,11... | collective-permute-start | bytes 786440 | tf_op jit(solution)/shard_map/ppermute | solution.py:24
  497.5 10.2 %collective-permute-start.45 = (bf16[256,512]{1,0:T(8,128)(2,1)}, bf16[256,512]{1,0:T(8,128)(2,1)S(1)}, u32[]{:S(2)}, u32[]{:S(2)}) collective-permute-start(bf16[256,512]{1,0:T(8,128)(2,1)} %collective-permute-done.41.refs_2_), channel_id=1, source_target_pairs={{0,1},{1,0},{2,3},{3,2},{4,5},{5,4},{6,7},{7,6},{8,9},{9,8},{10,11... | collective-permute-start | bytes 786440 | tf_op jit(solution)/shard_map/ppermute | solution.py:24
  519.9 16.5 %collective-permute-start.47 = (bf16[128,2048]{1,0:T(8,128)(2,1)}, bf16[128,2048]{1,0:T(8,128)(2,1)S(1)}, u32[]{:S(2)}, u32[]{:S(2)}) collective-permute-start(bf16[128,2048]{1,0:T(8,128)(2,1)} %attend_out.12), channel_id=1, source_target_pairs={{0,8},{8,16},{16,24},{1,9},{9,17},{17,25},{2,10},{10,18},{18,26},{... | collective-permute-start | bytes 1572872 | tf_op jit(solution)/shard_map/ppermute | solution.py:255
  541.2 14.7 %collective-permute-start.48 = (bf16[256,512]{1,0:T(8,128)(2,1)}, bf16[256,512]{1,0:T(8,128)(2,1)S(1)}, u32[]{:S(2)}, u32[]{:S(2)}) collective-permute-start(bf16[256,512]{1,0:T(8,128)(2,1)} %get-tuple-element.57.refs_0_), channel_id=1, source_target_pairs={{0,4},{1,5},{2,6},{3,7},{4,0},{5,1},{6,2},{7,3},{8,12},{9,13},{10,... | collective-permute-start | bytes 786440 | tf_op jit(solution)/shard_map/ppermute | solution.py:24
  541.4 15.3 %collective-permute-start.49 = (bf16[256,512]{1,0:T(8,128)(2,1)}, bf16[256,512]{1,0:T(8,128)(2,1)S(1)}, u32[]{:S(2)}, u32[]{:S(2)}) collective-permute-start(bf16[256,512]{1,0:T(8,128)(2,1)} %get-tuple-element.57.refs_0_), channel_id=1, source_target_pairs={{0,2},{1,3},{2,0},{3,1},{4,6},{5,7},{6,4},{7,5},{8,10},{9,11},{10,... | collective-permute-start | bytes 786440 | tf_op jit(solution)/shard_map/ppermute | solution.py:24
  556.0 10.0 %collective-permute-start.51 = (bf16[256,512]{1,0:T(8,128)(2,1)S(1)}, bf16[256,512]{1,0:T(8,128)(2,1)S(1)}, u32[]{:S(2)}, u32[]{:S(2)}) collective-permute-start(bf16[256,512]{1,0:T(8,128)(2,1)S(1)} %copy-done.12), channel_id=1, source_target_pairs={{0,1},{1,0},{2,3},{3,2},{4,5},{5,4},{6,7},{7,6},{8,9},{9,8},{10,11... | collective-permute-start | bytes 786440 | tf_op jit(solution)/shard_map/ppermute | solution.py:24
  556.5 9.5 %collective-permute-start.52 = (bf16[256,512]{1,0:T(8,128)(2,1)S(1)}, bf16[256,512]{1,0:T(8,128)(2,1)S(1)}, u32[]{:S(2)}, u32[]{:S(2)}) collective-permute-start(bf16[256,512]{1,0:T(8,128)(2,1)S(1)} %collective-permute-done.48.refs_1_), channel_id=1, source_target_pairs={{0,1},{1,0},{2,3},{3,2},{4,5},{5,4},{6,7},{7,6},{8,9},{9,8},{10,11... | collective-permute-start | bytes 786440 | tf_op jit(solution)/shard_map/ppermute | solution.py:24
  556.6 9.4 %collective-permute-start.53 = (bf16[256,512]{1,0:T(8,128)(2,1)S(1)}, bf16[256,512]{1,0:T(8,128)(2,1)S(1)}, u32[]{:S(2)}, u32[]{:S(2)}) collective-permute-start(bf16[256,512]{1,0:T(8,128)(2,1)S(1)} %collective-permute-done.49.refs_2_), channel_id=1, source_target_pairs={{0,1},{1,0},{2,3},{3,2},{4,5},{5,4},{6,7},{7,6},{8,9},{9,8},{10,11... | collective-permute-start | bytes 786440 | tf_op jit(solution)/shard_map/ppermute | solution.py:24
  (83 other events, 640.8 us)
Sparse Core Ops, SparseCore 0:
  9.0 118.2 all-gather.2
  128.9 91.7 all-gather.4
